TPU v7x, 128 devices: a whole 4x4x4 slice. The times are simulated.
128 devices in a mesh: pole: 4 (over x_hi, core), row: 4 (over y), col: 8 (over x_lo, z).
Axes of the slice: x: 4 (x_hi: 2, x_lo: 2; x = x_hi * 2 + x_lo), y: 4, z: 4, core: 2. Of those that a mesh axis runs over, the one named last changes fastest.
Arguments:
- inverse: bfloat16 [4, 2, 4096, 4096], P('pole', None, 'row', 'col'), may hold values from -0.0625 to 0.0625
- factor: bfloat16 [4, 1, 2048, 1024], P('pole', None, ('row', 'col')), may hold values from -1.796875 to 1.796875
- dinv: float32 [512, 4, 1, 2, 512], P(('row', 'col'), 'pole'), may hold values from -6 to 6
- ancestors: int32 [1, 16], replicated, may hold values from 0 to 31, as said below
- owner: int32 [2048, 1], P(('row', 'col')), may hold values from 0 to 127; in each aligned block of 64 rows (0 to 63, 64 to 127, ...) at most 2 rows name the same one
- weight_table: float32 [2, 16], replicated, may hold values from -4 to 4
- pole_slot: int32 [4], P('pole'), may hold values from 0 to 15
Outputs:
- inverse_column: float32 [4096, 4, 1, 2, 512], P(('row', 'col'), 'pole')
- diag_inverse: float32 [512, 4, 1, 2, 512], P(('row', 'col'), 'pole')
- density_diag: float32 [512, 1, 512], P(('row', 'col'))
- tile_density: float32 [128, 8, 128], P(('pole', 'row', 'col'))
Inputs may be any that keep to these rules, and one draw needn't show every extreme that they name: `ancestors`: each row lists 16 distinct block numbers in increasing order. In the rows of one device (64 rows of owner) no tile is named more than 2 times.
All inputs are finite; a program needn't handle non-finite values.
Results may differ from a plain program's by a relative error of at most 0.0028.
Values may be sent and summed in bfloat16 or wider, within the bound.
A program may use at most 64 MiB of HBM per device.

v0:
```python
import jax
import jax.numpy as jnp
from jax import lax
from jax.sharding import Mesh
from jax.sharding import PartitionSpec as P

A = 4096
S = 512
SN = 1
BS = 128
NSEL = 16
BR = 8
BC = 128
NWEIGHT = 16
COL = ("col_0", "col_1")
ROW_COL = ("row", "col_0", "col_1")
POLE_ROW_COL = ("pole", "row", "col_0", "col_1")


precise = lax.Precision.HIGHEST


def joined_along(blocks, dim):
    blocks = jnp.moveaxis(blocks, 0, dim)
    dims = blocks.shape
    return blocks.reshape(*dims[:dim], dims[dim] * dims[dim + 1], *dims[dim + 2 :])


def all_blocks(x, axes, turns):
    blocks = x
    for k in turns:
        blocks = lax.all_gather(blocks, axes[k])
    done = turns[::-1]
    back = [done.index(k) for k in range(len(axes))]
    blocks = blocks.transpose(*back, *range(len(axes), blocks.ndim))
    return blocks.reshape(-1, *x.shape)


def gathered_by_axis(x, axes, turns, dim):
    return joined_along(all_blocks(x, axes, turns), dim)


def split_up(x, dim, size):
    dims = x.shape
    blocks = x.reshape(*dims[:dim], size, dims[dim] // size, *dims[dim + 1 :])
    return jnp.moveaxis(blocks, dim, 0)


def sent_and_summed(x, axis, dim):
    size = lax.axis_size(axis)
    blocks = lax.all_to_all(split_up(x, dim, size), axis, 0, 0, tiled=True)
    return jnp.sum(blocks, axis=0)


def copy_for_each(x, axis):
    size = lax.axis_size(axis)
    return lax.all_to_all(jnp.broadcast_to(x[None], (size, *x.shape)), axis, 0, 0, tiled=True)


def over_copies(x, axis):
    return copy_for_each(x, axis).sum(axis=0)


def body(inverse, factor, dinv, ancestors, owner, weight_table, pole_slot):
    members = inverse.shape[0]
    col_count = lax.axis_size(COL)
    grid_count = lax.axis_size("row") * col_count
    tile_count = lax.axis_size("pole") * grid_count
    rows_here = A // grid_count
    position = lax.axis_index(ROW_COL)
    gathered = gathered_by_axis(factor, ROW_COL, (1, 0, 2), 2)
    compact = gathered.reshape(members, SN, NSEL, BS, 2, S)
    swapped = jnp.concatenate([-compact[:, :, :, :, 1:, :], compact[:, :, :, :, :1, :]], axis=4)
    row_blocks = position * (rows_here // BS) + jnp.arange(rows_here // BS)
    match_rows = row_blocks[None, :, None] == ancestors[:, None, :]
    pick_rows = match_rows.astype(jnp.bfloat16)
    factor_rows = jnp.einsum(
        "kjn,pknbcs->jbpkcs", pick_rows, compact, preferred_element_type=jnp.float32
    )
    factor_rows = factor_rows.astype(jnp.bfloat16).reshape(rows_here, members, SN, 2, S)
    choose_map = (jnp.arange(NWEIGHT)[None, :] == pole_slot[:, None]).astype(jnp.float32)
    weights = jnp.dot(choose_map, weight_table.T, precision=precise)
    row_strip = lax.all_to_all(inverse, COL, split_axis=2, concat_axis=3, tiled=True)
    strip_blocks = row_strip.reshape(members, 2, rows_here, A // BS, BS)
    chosen = jnp.take(strip_blocks[0], ancestors[0], axis=2).reshape(2, rows_here, NSEL * BS)
    plain_part = compact[0, 0].reshape(NSEL * BS, 2 * S)
    turned_part = swapped[0, 0].reshape(NSEL * BS, 2 * S)
    per_super = [
        jnp.dot(chosen[0], plain_part, preferred_element_type=jnp.float32)
        + jnp.dot(chosen[1], turned_part, preferred_element_type=jnp.float32)
    ]
    stacked = [jnp.stack(per_super, axis=1)]
    summed = jnp.stack(stacked, axis=1)
    keep_rows = jnp.any(match_rows, axis=2).T[:, None, None, :, None]
    summed_blocks = summed.reshape(rows_here // BS, BS, members, SN, 2 * S)
    column_out = jnp.where(keep_rows, -summed_blocks, 0.0).reshape(rows_here, members, SN, 2, S)
    rounded = summed.astype(jnp.bfloat16)
    rounded_turned = jnp.concatenate([-rounded[:, :, :, S:], rounded[:, :, :, :S]], axis=3)
    left_real = factor_rows[:, :, :, 0, :]
    left_imag = factor_rows[:, :, :, 1, :]
    product = jnp.einsum("apkc,apkx->cpkx", left_real, rounded, preferred_element_type=jnp.float32)
    mixed = sent_and_summed(
        product
        + jnp.einsum(
            "apkc,apkx->cpkx", left_imag, rounded_turned, preferred_element_type=jnp.float32
        ),
        ROW_COL,
        0,
    )
    diag_inverse = dinv + mixed.reshape(S // grid_count, members, SN, 2, S)
    weight_real = weights[:, 0][None, :, None, None]
    weight_imag = weights[:, 1][None, :, None, None]
    diag_share = jnp.sum(
        weight_real * diag_inverse[:, :, :, 1] + weight_imag * diag_inverse[:, :, :, 0], axis=1
    )
    density_diag = over_copies(diag_share, "pole")
    column_share = jnp.sum(
        weight_real * column_out[:, :, :, 1] + weight_imag * column_out[:, :, :, 0], axis=1
    )
    block_total = owner.shape[0]
    pieces = (
        column_share.reshape(rows_here // BR, BR, SN, S // BC, BC)
        .transpose(0, 2, 3, 1, 4)
        .reshape(block_total, BR * BC)
    )
    target_tile = owner[:, 0]
    shared = target_tile[:, None] == target_tile[None, :]
    earlier = jnp.arange(block_total)[None, :] < jnp.arange(block_total)[:, None]
    slot_index = jnp.sum(jnp.logical_and(shared, earlier).astype(jnp.int32), axis=1)
    capacity = max(2, 2 * block_total // tile_count)
    target_slot = target_tile * capacity + slot_index
    send_map = (jnp.arange(tile_count * capacity)[:, None] == target_slot[None, :]).astype(
        jnp.float32
    )
    outgoing = jnp.dot(send_map, pieces, precision=precise).reshape(tile_count, capacity, BR * BC)
    arrived = lax.all_to_all(outgoing, POLE_ROW_COL, split_axis=0, concat_axis=0, tiled=True)
    tile_sum = jnp.sum(arrived, axis=(0, 1)).reshape(1, BR, BC)
    return (column_out, diag_inverse, density_diag, tile_sum)


def solution(mesh):
    split = Mesh(
        mesh.devices.reshape(mesh.shape["pole"], mesh.shape["row"], 2, 4),
        ("pole", "row", "col_0", "col_1"),
    )
    in_specs = (
        P("pole", None, "row", COL),
        P("pole", None, ROW_COL, None),
        P(ROW_COL, "pole", None, None, None),
        P(),
        P(ROW_COL, None),
        P(),
        P("pole"),
    )
    out_specs = (
        P(ROW_COL, "pole", None, None, None),
        P(ROW_COL, "pole", None, None, None),
        P(ROW_COL, None, None),
        P(POLE_ROW_COL, None, None),
    )
    return jax.shard_map(body, mesh=split, in_specs=in_specs, out_specs=out_specs, check_vma=False)
```

profile of v0, /device:TPU:1, one launch (start us, length us, event | category | flops | bytes accessed | tf_op | source)
XLA Modules:
  0.0 240.0 jit_solution(13185274059475193080)
XLA Ops:
  7.2 7.7 %all-gather = bf16[2,1,64,1024]{3,2,1,0:T(8,128)(2,1)} all-gather(bf16[1,1,64,1024]{3,2,1,0:T(8,128)(2,1)} %param.8), channel_id=2, replica_groups=mesh['pole'=4,'row'=4,'col_0'=2,'col_1'=4] {'col_0'}, dimensions={0}, use_global_device_ids=true | all-gather | bytes 393216 | tf_op jit(solution)/shard_map/all_gather | solution.py:32
  15.0 24.8 %all-gather.6.cloned.1.call-done = bf16[8,1,64,1024]{3,2,1,0:T(8,128)(2,1)} async-done(((bf16[2,1,64,1024]{3,2,1,0:T(8,128)(2,1)}), bf16[8,1,64,1024]{3,2,1,0:T(8,128)(2,1)}) %all-gather.6.cloned.1.call-update) | async-done | bytes 1048592 | tf_op jit(solution)/shard_map/all_gather | solution.py:32
  39.8 5.1 %copy.47 = bf16[1,2,1024,512]{3,1,0,2:T(2,128)(2,1)} copy(bf16[1,2,1024,512]{3,2,1,0:T(8,128)(2,1)} %param.7) | data formatting | bytes 4194304 | tf_op args[0]
  44.9 5.1 %all-to-all-start = ((bf16[1,2,1024,512]{3,1,0,2:T(2,128)(2,1)}), bf16[1,2,1024,512]{3,1,0,2:T(2,128)(2,1)S(1)}, u32[]{:S(2)}, u32[]{:S(2)}) async-start(bf16[1,2,1024,512]{3,1,0,2:T(2,128)(2,1)} %copy.47), calls=%async_computation | async-start | bytes 4194304 | tf_op jit(solution)/shard_map/all_to_all | solution.py:83
  50.0 0.6 compare_reduce_fusion
  50.6 29.1 %all-to-all-done = bf16[1,2,1024,512]{3,1,0,2:T(2,128)(2,1)S(1)} async-done(((bf16[1,2,1024,512]{3,1,0,2:T(2,128)(2,1)}), bf16[1,2,1024,512]{3,1,0,2:T(2,128)(2,1)S(1)}, u32[]{:S(2)}, u32[]{:S(2)}) %all-to-all-start) | async-done | bytes 2097184 | tf_op jit(solution)/shard_map/all_to_all | solution.py:83
  79.8 1.7 copy.48
  81.4 3.0 %copy.49 = bf16[1,2,128,8,512]{2,4,3,1,0:T(8,128)(2,1)S(1)} copy(bf16[1,2,128,8,512]{4,2,3,1,0:T(8,128)(2,1)} %bitcast.102) | data formatting | bytes 4194304 | tf_op jit(solution)/shard_map/all_to_all | solution.py:83
  84.5 2.8 %copy.50 = bf16[2,128,32,128]{3,1,2,0:T(8,128)(2,1)} copy(bf16[2,128,32,128]{1,3,2,0:T(8,128)(2,1)S(1)} %bitcast.103) | data formatting | bytes 4194304 | tf_op jit(solution)/shard_map/squeeze;reshape | solution.py:85
  87.2 2.3 gather_fusion
  89.6 0.2 select_bitcast_fusion
  89.7 0.1 fusion.22
  89.8 0.3 copy.54
  90.1 0.3 copy.51
  90.4 20.1 %all-gather.8.cloned.1.call-done = bf16[16,2,1,1,64,1024]{5,4,3,2,1,0:T(8,128)(2,1)} async-done(((bf16[4,2,1,1,64,1024]{5,4,3,2,1,0:T(8,128)(2,1)}), bf16[16,2,1,1,64,1024]{5,4,3,2,1,0:T(8,128)(2,1)}) %all-gather.8.cloned.1.call-update) | async-done | bytes 4194320 | tf_op jit(solution)/shard_map/all_gather | solution.py:32
  110.5 4.9 %copy.53 = bf16[4,2,4,1,1,64,1024]{6,5,2,1,0,4,3:T(8,128)(2,1)} copy(bf16[4,2,4,1,1,64,1024]{6,5,1,0,2,4,3:T(8,128)(2,1)} %bitcast.104) | data formatting | bytes 8388608 | tf_op jit(solution)/shard_map/transpose | solution.py:35
  115.4 7.8 %reshape.223 = bf16[16,128,2,512]{3,2,1,0:T(2,128)(2,1)} reshape(bf16[4,2,4,1,1,64,1024]{6,5,2,1,0,4,3:T(8,128)(2,1)} %copy.53) | data formatting | bytes 8388608 | tf_op jit(solution)/shard_map/reshape.8
  123.2 7.8 %reshape_reshape_transpose_reshape.3 = bf16[1,1,16,128,2,512]{5,4,3,2,1,0:T(2,128)(2,1)} reshape(bf16[4,2,4,1,1,64,1024]{6,5,2,1,0,4,3:T(8,128)(2,1)} %copy.53) | data formatting | bytes 8388608 | tf_op jit(solution)/shard_map/reshape;reshape;transpose;reshape | solution.py:72
  131.0 4.9 %fusion = bf16[1,128,2,512]{3,0,2,1:T(2,128)(2,1)S(1)} fusion(bf16[16,128,2,512]{3,2,1,0:T(2,128)(2,1)} %reshape.223, s32[1,16]{1,0:T(1,128)S(1)} %copy-done.6, s32[]{:T(128)S(6)} %add.75), kind=kOutput, calls=%fused_computation.3 | convolution fusion | flops 4194320 | bytes 4456516 | tf_op jit(solution)/shard_map/kjn,pknbcs->jbpkcs/dot_general | solution.py:77
  135.9 0.1 copy.76
  136.0 9.3 %slice_negate_fusion = (bf16[1,1,16,128,1,512]{5,4,3,2,1,0:T(2,128)(2,1)S(1)}, bf16[1,1,16,128,1,512]{5,4,3,2,1,0:T(2,128)(2,1)S(1)}) fusion(bf16[1,1,16,128,2,512]{5,4,3,2,1,0:T(2,128)(2,1)S(1)} %copy-done.2), kind=kLoop, calls=%fused_computation.1 | loop fusion | flops 1048576 | bytes 8388608 | tf_op jit(solution)/shard_map/neg | solution.py:73
  145.4 9.7 %pad_maximum_fusion = bf16[1,1,16,128,2,512]{5,4,3,2,1,0:T(2,128)(2,1)S(1)} fusion(bf16[1,1,16,128,1,512]{5,4,3,2,1,0:T(2,128)(2,1)S(1)} %get-tuple-element.25, bf16[1,1,16,128,1,512]{5,4,3,2,1,0:T(2,128)(2,1)S(1)} %get-tuple-element.24), kind=kLoop, calls=%fused_computation.2 | loop fusion | flops 8388608 | bytes 8388608 | tf_op jit(solution)/shard_map/concatenate | solution.py:73
  155.0 1.2 copy.68
  156.2 1.0 copy-done.1
  157.2 0.8 fusion.24
  158.0 0.8 convolution_add_fusion.1
  158.8 0.7 convert_bitcast_fusion
  159.5 0.5 fusion.6
  160.0 1.8 convolution_add_fusion
  161.8 5.8 %all-to-all-start.1 = ((f32[32,16,1,1,1024]{4,1,3,2,0:T(8,128)}), f32[32,16,1,1,1024]{4,1,3,2,0:T(8,128)S(1)}, u32[]{:S(2)}, u32[]{:S(2)}) async-start(f32[32,16,1,1,1024]{4,1,3,2,0:T(8,128)} %bitcast.101), calls=%async_computation.1 | async-start | bytes 4194304 | tf_op jit(solution)/shard_map/all_to_all | solution.py:51
  168.3 0.1 fusion.15
  168.4 0.6 fusion.23
  169.0 0.2 convert_reduce_fusion
  169.2 0.4 reshape.222
  169.7 1.7 fusion.3
  171.4 0.7 fusion.8
  172.1 1.8 copy.60
  173.9 21.7 %all-to-all-done.1 = f32[32,16,1,1,1024]{4,1,3,2,0:T(8,128)S(1)} async-done(((f32[32,16,1,1,1024]{4,1,3,2,0:T(8,128)}), f32[32,16,1,1,1024]{4,1,3,2,0:T(8,128)S(1)}, u32[]{:S(2)}, u32[]{:S(2)}) %all-to-all-start.1) | async-done | bytes 2097184 | tf_op jit(solution)/shard_map/all_to_all | solution.py:51
  195.6 8.0 %all-to-all-start.3 = ((f32[128,2,1024]{2,1,0:T(2,128)}), f32[128,2,1024]{2,1,0:T(2,128)S(1)}, u32[]{:S(2)}, u32[]{:S(2)}) async-start(f32[128,2,1024]{2,1,0:T(2,128)} %copy.60), calls=%async_computation.3 | async-start | bytes 2097152 | tf_op jit(solution)/shard_map/all_to_all | solution.py:136
  203.6 0.1 reduce_sum.37
  203.7 0.1 reshape.229
  203.8 1.4 fusion.10
  205.2 16.9 %all-to-all-done.3 = f32[128,2,1024]{2,1,0:T(2,128)S(1)} async-done(((f32[128,2,1024]{2,1,0:T(2,128)}), f32[128,2,1024]{2,1,0:T(2,128)S(1)}, u32[]{:S(2)}, u32[]{:S(2)}) %all-to-all-start.3) | async-done | bytes 1048608 | tf_op jit(solution)/shard_map/all_to_all | solution.py:136
  222.1 0.7 broadcast_in_dim.39
  222.8 4.7 %all-to-all-start.2 = ((f32[4,16,1,512]{3,1,2,0:T(8,128)}), f32[4,16,1,512]{3,1,2,0:T(8,128)S(1)}, u32[]{:S(2)}, u32[]{:S(2)}) async-start(f32[4,16,1,512]{3,1,2,0:T(8,128)} %broadcast_in_dim.39), calls=%async_computation.2 | async-start | bytes 262144 | tf_op jit(solution)/shard_map/all_to_all | solution.py:57
  227.4 1.0 reduce_sum.50
  228.4 4.1 %all-to-all-done.2 = f32[4,16,1,512]{3,1,2,0:T(8,128)S(1)} async-done(((f32[4,16,1,512]{3,1,2,0:T(8,128)}), f32[4,16,1,512]{3,1,2,0:T(8,128)S(1)}, u32[]{:S(2)}, u32[]{:S(2)}) %all-to-all-start.2) | async-done | bytes 131104 | tf_op jit(solution)/shard_map/all_to_all | solution.py:57
  232.5 0.6 copy.63
  (30 shorter events, 0.3 us)
Async XLA Ops:
  7.2 161.1 %copy-start = (f32[2,16]{1,0:T(2,128)S(1)}, f32[2,16]{1,0:T(2,128)}, u32[]{:S(2)}) copy-start(f32[2,16]{1,0:T(2,128)} %param.12) | copy-start | bytes 388
  7.2 32.6 %all-gather.6.cloned.1.call-start = ((), (), s32[]{:S(2)}) async-start(), calls=%async_computation.4 | async-start | bytes 1310720 | tf_op jit(solution)/shard_map/all_gather | solution.py:32
  14.9 95.6 %all-gather.8.cloned.1.call-start = ((), (), s32[]{:S(2)}) async-start(), calls=%async_computation.5 | async-start | bytes 5242880 | tf_op jit(solution)/shard_map/all_gather | solution.py:32
  39.8 10.1 %copy-start.6 = (s32[1,16]{1,0:T(1,128)S(1)}, s32[1,16]{1,0:T(1,128)}, u32[]{:S(2)}) copy-start(s32[1,16]{1,0:T(1,128)} %param.10) | copy-start | bytes 196
  44.9 34.8 %all-to-all-start = ((bf16[1,2,1024,512]{3,1,0,2:T(2,128)(2,1)}), bf16[1,2,1024,512]{3,1,0,2:T(2,128)(2,1)S(1)}, u32[]{:S(2)}, u32[]{:S(2)}) async-start(bf16[1,2,1024,512]{3,1,0,2:T(2,128)(2,1)} %copy.47), calls=%async_computation | async-start | bytes 4194304 | tf_op jit(solution)/shard_map/all_to_all | solution.py:83
  131.0 5.0 %copy-start.2 = (bf16[1,1,16,128,2,512]{5,4,3,2,1,0:T(2,128)(2,1)S(1)}, bf16[1,1,16,128,2,512]{5,4,3,2,1,0:T(2,128)(2,1)}, u32[]{:S(2)}) copy-start(bf16[1,1,16,128,2,512]{5,4,3,2,1,0:T(2,128)(2,1)} %reshape_reshape_transpose_reshape.3) | copy-start | bytes 12582916
  155.0 2.2 copy-start.1
  160.0 9.0 %copy-start.7 = (s32[64,1]{0,1:T(1,128)S(1)}, s32[64,1]{0,1:T(1,128)}, u32[]{:S(2)}) copy-start(s32[64,1]{0,1:T(1,128)} %param.11) | copy-start | bytes 772
  161.8 33.8 %all-to-all-start.1 = ((f32[32,16,1,1,1024]{4,1,3,2,0:T(8,128)}), f32[32,16,1,1,1024]{4,1,3,2,0:T(8,128)S(1)}, u32[]{:S(2)}, u32[]{:S(2)}) async-start(f32[32,16,1,1,1024]{4,1,3,2,0:T(8,128)} %bitcast.101), calls=%async_computation.1 | async-start | bytes 4194304 | tf_op jit(solution)/shard_map/all_to_all | solution.py:51
  169.6 26.0 %copy-start.3 = (f32[128,1,1,2,512]{4,3,0,2,1:T(2,128)}, f32[128,1,1,2,512]{4,3,0,2,1:T(2,128)S(1)}, u32[]{:S(2)}) copy-start(f32[128,1,1,2,512]{4,3,0,2,1:T(2,128)S(1)} %reshape.222) | copy-start | bytes 1572868
  171.3 32.4 %copy-start.5 = (f32[16,1,1,2,512]{4,3,2,1,0:T(2,128)S(1)}, f32[16,1,1,2,512]{4,3,2,1,0:T(2,128)}, u32[]{:S(2)}) copy-start(f32[16,1,1,2,512]{4,3,2,1,0:T(2,128)} %param.9) | copy-start | bytes 196612
  195.6 26.5 %all-to-all-start.3 = ((f32[128,2,1024]{2,1,0:T(2,128)}), f32[128,2,1024]{2,1,0:T(2,128)S(1)}, u32[]{:S(2)}, u32[]{:S(2)}) async-start(f32[128,2,1024]{2,1,0:T(2,128)} %copy.60), calls=%async_computation.3 | async-start | bytes 2097152 | tf_op jit(solution)/shard_map/all_to_all | solution.py:136
  203.8 29.4 %copy-start.4 = (f32[16,1,1,2,512]{4,3,0,2,1:T(2,128)}, f32[16,1,1,2,512]{4,3,0,2,1:T(2,128)S(1)}, u32[]{:S(2)}) copy-start(f32[16,1,1,2,512]{4,3,0,2,1:T(2,128)S(1)} %bitcast_add_fusion) | copy-start | bytes 196612
  222.8 9.8 %all-to-all-start.2 = ((f32[4,16,1,512]{3,1,2,0:T(8,128)}), f32[4,16,1,512]{3,1,2,0:T(8,128)S(1)}, u32[]{:S(2)}, u32[]{:S(2)}) async-start(f32[4,16,1,512]{3,1,2,0:T(8,128)} %broadcast_in_dim.39), calls=%async_computation.2 | async-start | bytes 262144 | tf_op jit(solution)/shard_map/all_to_all | solution.py:57
Sparse Core Ops, SparseCore 0:
  15.1 24.6 all-gather.5
  41.5 69.0 all-gather.7
where the time goes:
time: 241 us; the launch traced here: 240 us
  waiting for transfers between devices  117 us (49%)
  local copies, waits for them, and re-layouts  42.6 us (18%)
  other arithmetic  24.9 us (10%)
  starting transfers between devices  23.6 us (10%)
  between operations  15 us (6%)
  matrix products  9.52 us (4%)
  blocking collectives  7.7 us (3%)
    all_gather x2, waiting for transfers between devices, all_blocks(): blocks = lax.all_gather(blocks, axes[k])  44.9 us
    all_to_all x1, waiting for transfers between devices, body(): lax.all_to_all(inverse, COL, split_axis=2, concat_axis=3, tiled=True)  29.1 us
    all_to_all x1, waiting for transfers between devices, sent_and_summed(): blocks = lax.all_to_all(split_up(x, dim, size), axis, 0, 0, tiled=True)  21.7 us
    all_to_all x1, waiting for transfers between devices, body(): lax.all_to_all(outgoing, POLE_ROW_COL, split_axis=0, concat_axis=0, tiled...  16.9 us
    concatenate x1, other arithmetic, body(): jnp.concatenate([-compact[:, :, :, :, 1:, :], compact[:, :, :, :, :1, :]]...  9.67 us
    neg x1, other arithmetic, body(): -compact[:, :, :, :, 1:, :]  9.33 us
    all_to_all x1, starting transfers between devices, body(): lax.all_to_all(outgoing, POLE_ROW_COL, split_axis=0, concat_axis=0, tiled...  7.96 us
    unnamed x20, local copies, waits for them, and re-layouts  7.95 us
  transfers between devices with their start and end apart: 6, of which 6 were waited for; matrix products, arithmetic and copies ran while one was open for 10% of the time, Pallas kernels for 0%

commit v1 on v0

v1 whole, which is shorter than its diff:
```python
import jax
import jax.numpy as jnp
from jax import lax
from jax.experimental import pallas as pl
from jax.experimental.pallas import tpu as pltpu
from jax.sharding import PartitionSpec as P

S = 512
BS = 128
NSEL = 16
NWEIGHT = 16
ROWS = 4
COLS = 8
POLES = 4
GRID = ROWS * COLS
LROWS = NSEL * BS // GRID
HALF = LROWS // 2
MESH = pl.DeviceIdType.MESH
BF = jnp.bfloat16
F32 = jnp.float32


def kernel(
    inverse,
    factor,
    dinv,
    ancestors,
    owner,
    table,
    slot,
    column_out,
    diag_out,
    density_out,
    tile_out,
    lbuf,
    gbuf,
    abuf,
    acc,
    col_buf,
    ysend,
    yrecv,
    dsend,
    drecv,
    pick,
    tsend,
    trecv,
    psend,
    precv,
    qsend,
    qrecv,
    local_sem,
    l_send,
    l_recv,
    h_send,
    h_recv,
    g_send,
    g_recv,
    y_send,
    y_recv,
    d_send,
    d_recv,
    t_send,
    t_recv,
    p_send,
    p_recv,
    q_send,
    q_recv,
    out_sem,
):
    pole, row, col = lax.axis_index("pole"), lax.axis_index("row"), lax.axis_index("col")
    side, depth = col // 4, col % 4
    me = row * COLS + col

    def plane(ds, dz):
        return ((side + ds) % 2) * 4 + (depth + dz) % 4

    def up(k):
        return (row + k) % ROWS

    def remote(src, dst, send, recv, to):
        return pltpu.make_async_remote_copy(
            src_ref=src,
            dst_ref=dst,
            send_sem=send,
            recv_sem=recv,
            device_id=to,
            device_id_type=MESH,
        )

    sends = []

    def go(copy):
        copy.start()
        sends.append(copy)

    own_factor = pltpu.make_async_copy(
        factor, lbuf.at[me // 2, pl.ds((me % 2) * LROWS, LROWS)], local_sem.at[0]
    )
    own_factor.start()

    def piece(c, k):
        return inverse.at[:, pl.ds(c * BS, BS), pl.ds(k * BS, BS)]

    for k in range(4):
        pltpu.make_async_copy(piece(col, k), gbuf.at[col * 4 + k], local_sem.at[1]).start()

    barrier = pltpu.get_barrier_semaphore()
    others = [(ds, dz) for ds in (0, 1) for dz in (0, 1, 3, 2) if (ds, dz) != (0, 0)]
    for ds, dz in others:
        pl.semaphore_signal(
            barrier, inc=1, device_id=(pole, row, plane(ds, dz)), device_id_type=MESH
        )
    for k in (1, 3, 2):
        pl.semaphore_signal(barrier, inc=1, device_id=(pole, up(k), col), device_id_type=MESH)
    for k in range(1, POLES):
        pl.semaphore_signal(
            barrier, inc=1, device_id=((pole + k) % POLES, row, col), device_id_type=MESH
        )
    pl.semaphore_wait(barrier, len(others) + ROWS - 1 + POLES - 1)
    own_factor.wait()

    def block(r, c):
        return lbuf.at[r * 4 + c // 2, pl.ds((c % 2) * LROWS, LROWS)]

    def half(r, c, part):
        return lbuf.at[r * 4 + c // 2, pl.ds((c % 2) * LROWS + part * HALF, HALF)]

    count = [0]

    def send_block(r, c, to):
        k = count[0]
        count[0] += 1
        go(remote(block(r, c), block(r, c), l_send.at[k], l_recv.at[r * COLS + c], to))

    def wait_block(r, c):
        remote(
            block(r, c), block(r, c), l_send.at[0], l_recv.at[r * COLS + c], (pole, row, col)
        ).wait_recv()

    halves = [0]

    def send_half(r, c, part, to):
        k = halves[0]
        halves[0] += 1
        go(
            remote(
                half(r, c, part), half(r, c, part), h_send.at[k], h_recv.at[part, c], to
            )
        )

    def wait_half(r, c, part):
        remote(
            half(r, c, part), half(r, c, part), h_send.at[0], h_recv.at[part, c], (pole, row, col)
        ).wait_recv()

    def along_rows(c):
        send_block(row, c, (pole, up(1), col))
        send_block(row, c, (pole, up(3), col))

    def pass_on(c):
        wait_block(up(3), c)
        send_half(up(3), c, 0, (pole, up(1), col))
        wait_block(up(1), c)
        send_half(up(1), c, 1, (pole, up(3), col))

    send_block(row, col, (pole, row, plane(1, 0)))
    along_rows(col)
    for dz in (1, 3, 2):
        send_block(row, col, (pole, row, plane(0, dz)))
    facing = plane(1, 0)
    wait_block(row, facing)
    along_rows(facing)
    for dz in (1, 3, 2):
        send_block(row, facing, (pole, row, plane(0, dz)))

    for n, (ds, dz) in enumerate(((1, 2), (1, 1), (1, 3), (1, 0), (0, 2), (0, 1), (0, 3))):
        c = plane(ds, dz)
        for k in range(4):
            remote(
                piece(c, k), gbuf.at[col * 4 + k], g_send.at[n], g_recv.at[col], (pole, row, c)
            ).start()

    def strip(c, n):
        four = gbuf.at[pl.ds(c * 4, 4)]
        return remote(four, four, g_send.at[n], g_recv.at[c], (pole, row, col))

    order = [plane(0, 0), plane(1, 0), plane(0, 1), plane(0, 3)]
    order += [plane(1, 1), plane(1, 3), plane(0, 2), plane(1, 2)]
    for k in (2, 3):
        wait_block(row, order[k])
        along_rows(order[k])
    pass_on(order[0])
    pass_on(order[1])
    for k in (4, 5):
        wait_block(row, order[k])
        along_rows(order[k])
    pass_on(order[2])
    for k in (6, 7):
        wait_block(row, order[k])
        along_rows(order[k])
    for k in range(3, 8):
        pass_on(order[k])

    lane = lax.broadcasted_iota(jnp.int32, (64, 512), 1)
    owner_index = lax.broadcasted_iota(jnp.int32, (64, 512), 0)
    mine = ((lane & 127) >> 3) * 4 + (lane >> 7)
    target = owner[...]
    target = ((target & 31) * 32 + (target >> 5) * 8).astype(F32)
    spread = jnp.where(mine == owner_index, target, 0.0)
    key = jnp.sum(spread, axis=0, keepdims=True) + (lane[:1] & 7).astype(F32)
    position = lax.broadcasted_iota(jnp.int32, (1024, 512), 0).astype(F32)
    pick[...] = jnp.where(position == key, 1.0, 0.0).astype(BF)

    mine = gbuf.at[pl.ds(col * 4, 4)]
    pltpu.make_async_copy(mine, mine, local_sem.at[1]).wait()
    for ds, dz in others:
        strip(plane(ds, dz), 0).wait_recv()
    for i in range(NSEL):
        for part in range(2):
            abuf[i // 4, part * BS : (part + 1) * BS, (i % 4) * BS : (i % 4 + 1) * BS] = gbuf[
                ancestors[0, i], part
            ]

    def product(r):
        right = lbuf[pl.ds(r * 4, 4)].reshape(4 * BS, 2 * S)
        return jnp.dot(abuf[r], right, preferred_element_type=F32)

    acc[...] = product(row)
    acc[...] += product(up(1))
    acc[...] += product(up(3))
    for c in order:
        wait_half(up(2), c, 0)
        wait_half(up(2), c, 1)
    acc[...] += product(up(2))

    real = acc[:BS, :S] - acc[BS:, S:]
    imag = acc[:BS, S:] + acc[BS:, :S]

    chosen = jnp.int32(0)
    for i in range(NSEL):
        chosen += jnp.where(ancestors[0, i] == me, 1, 0)
    keep = lax.broadcast_in_dim(chosen, (BS, S), ()) > 0
    real = jnp.where(keep, real, 0.0)
    imag = jnp.where(keep, imag, 0.0)
    col_buf[0] = -real
    col_buf[1] = -imag
    column_copy = pltpu.make_async_copy(col_buf, column_out, out_sem)
    column_copy.start()
    for q in range(4):
        lanes = slice(q * BS, (q + 1) * BS)
        ysend[q] = jnp.concatenate([real[:, lanes], imag[:, lanes]], axis=1).astype(BF)
    for k in (2, 1, 3):
        r = up(k)
        go(remote(ysend.at[r], yrecv.at[row], y_send.at[k], y_recv.at[row], (pole, r, col)))
    yrecv[row] = ysend[row]

    weight_real = table[0, slot[0]]
    weight_imag = table[1, slot[0]]
    share = -(weight_real * imag + weight_imag * real)
    share = jnp.concatenate([share[:, q * BS : (q + 1) * BS] for q in range(4)], axis=0)
    high = share.astype(BF)
    low = (share - high.astype(F32)).astype(BF)
    tiles = jnp.dot(pick[...], jnp.concatenate([high, low], axis=1), preferred_element_type=F32)
    tiles = tiles[:, :BS] + tiles[:, BS:]
    tsend[...] = tiles.astype(BF).reshape(GRID, 32, BS)

    def to_position(k):
        to = (me + k) % GRID
        return to, (pole, to // COLS, to % COLS)

    def send_tiles(k, carry):
        to, device = to_position(k)
        remote(tsend.at[to], trecv.at[me], t_send, t_recv, device).start()
        return carry

    lax.fori_loop(1, GRID, send_tiles, 0)
    trecv[me] = tsend[me]

    for k in (1, 3, 2):
        r = up(k)
        remote(ysend.at[0], yrecv.at[r], y_send.at[0], y_recv.at[r], (pole, row, col)).wait_recv()
    lefts = []
    for r in range(4):
        b = r * COLS + col
        before = jnp.int32(0)
        for i in range(NSEL):
            before += jnp.where(ancestors[0, i] < b, 1, 0)
        before = jnp.minimum(before, NSEL - 1)
        lefts.append(lbuf[before])
    left = jnp.concatenate(lefts, axis=0)
    mixed = lax.dot_general(
        left, yrecv[...].reshape(4 * BS, 2 * BS), (((0,), (0,)), ((), ())), preferred_element_type=F32
    )
    diag_real = mixed[:S, :BS] - mixed[S:, BS:]
    diag_imag = mixed[:S, BS:] + mixed[S:, :BS]
    dsend[...] = (
        jnp.concatenate([diag_real, diag_imag], axis=1).astype(BF).reshape(GRID, S // GRID, 2 * BS)
    )

    def send_diag(k, carry):
        to, device = to_position(k)
        remote(dsend.at[to], drecv.at[me], d_send, d_recv, device).start()
        return carry

    lax.fori_loop(1, GRID, send_diag, 0)
    drecv[me] = dsend[me]

    most = pl.ds(0, GRID - 1)
    arrived = remote(tsend.at[most], trecv.at[most], t_send, t_recv, (pole, row, col))
    arrived.wait_recv()
    total = jnp.sum(trecv[...].astype(F32), axis=0)
    psend[...] = total.reshape(POLES, 8, BS)
    for k in range(1, POLES):
        p = (pole + k) % POLES
        go(remote(psend.at[p], precv.at[pole], p_send.at[k], p_recv.at[pole], (p, row, col)))
    precv[pole] = psend[pole]

    landed = remote(dsend.at[most], drecv.at[most], d_send, d_recv, (pole, row, col))
    landed.wait_recv()
    dreal, dimag = [], []
    for q in range(4):
        quarter = jnp.sum(drecv[q * COLS : (q + 1) * COLS].astype(F32), axis=0)
        dreal.append(quarter[:, :BS])
        dimag.append(quarter[:, BS:])
    dreal = jnp.concatenate(dreal, axis=1) + dinv[:, 0, :]
    dimag = jnp.concatenate(dimag, axis=1) + dinv[:, 1, :]
    diag_out[:, 0, :] = dreal
    diag_out[:, 1, :] = dimag
    qsend[...] = weight_real * dimag + weight_imag * dreal
    for k in range(1, POLES):
        p = (pole + k) % POLES
        go(remote(qsend, qrecv.at[pole], q_send.at[k], q_recv.at[pole], (p, row, col)))
    qrecv[pole] = qsend[...]
    for k in range(1, POLES):
        p = (pole + k) % POLES
        remote(psend.at[0], precv.at[p], p_send.at[0], p_recv.at[p], (pole, row, col)).wait_recv()
    tile_out[...] = jnp.sum(precv[...], axis=0)
    for k in range(1, POLES):
        p = (pole + k) % POLES
        remote(qsend, qrecv.at[p], q_send.at[0], q_recv.at[p], (pole, row, col)).wait_recv()
    density_out[...] = jnp.sum(qrecv[...], axis=0)

    arrived.wait_send()
    landed.wait_send()
    for copy in sends:
        copy.wait_send()
    for n in range(COLS - 1):
        strip(col, n).wait_send()
    column_copy.wait()


def body(inverse, factor, dinv, ancestors, owner, weight_table, pole_slot):
    vmem = pl.BlockSpec(memory_space=pltpu.VMEM)
    smem = pl.BlockSpec(memory_space=pltpu.SMEM)
    hbm = pl.BlockSpec(memory_space=pl.ANY)
    dma = pltpu.SemaphoreType.DMA
    column, diag, density, tile = pl.pallas_call(
        kernel,
        name="supernode",
        out_shape=(
            jax.ShapeDtypeStruct((2, BS, S), F32),
            jax.ShapeDtypeStruct((S // GRID, 2, S), F32),
            jax.ShapeDtypeStruct((S // GRID, S), F32),
            jax.ShapeDtypeStruct((8, BS), F32),
        ),
        in_specs=[hbm, hbm, vmem, smem, vmem, smem, smem],
        out_specs=(hbm, vmem, vmem, vmem),
        scratch_shapes=[
            pltpu.VMEM((NSEL, BS, 2 * S), BF),
            pltpu.VMEM((COLS * 4, 2, BS, BS), BF),
            pltpu.VMEM((4, 2 * BS, 4 * BS), BF),
            pltpu.VMEM((2 * BS, 2 * S), F32),
            pltpu.VMEM((2, BS, S), F32),
            pltpu.VMEM((4, BS, 2 * BS), BF),
            pltpu.VMEM((4, BS, 2 * BS), BF),
            pltpu.VMEM((GRID, S // GRID, 2 * BS), BF),
            pltpu.VMEM((GRID, S // GRID, 2 * BS), BF),
            pltpu.VMEM((1024, 512), BF),
            pltpu.VMEM((GRID, 32, BS), BF),
            pltpu.VMEM((GRID, 32, BS), BF),
            pltpu.VMEM((POLES, 8, BS), F32),
            pltpu.VMEM((POLES, 8, BS), F32),
            pltpu.VMEM((S // GRID, S), F32),
            pltpu.VMEM((POLES, S // GRID, S), F32),
            dma((2,)),
            dma((24,)),
            dma((GRID,)),
            dma((16,)),
            dma((2, COLS)),
            dma((7,)),
            dma((COLS,)),
            dma((4,)),
            dma((4,)),
            dma,
            dma,
            dma,
            dma,
            dma((POLES,)),
            dma((POLES,)),
            dma((POLES,)),
            dma((POLES,)),
            dma,
        ],
        compiler_params=pltpu.CompilerParams(
            collective_id=0, has_side_effects=True, vmem_limit_bytes=48 << 20
        ),
    )(
        inverse.reshape(2, 1024, 512),
        factor.reshape(LROWS, 2 * S),
        dinv.reshape(S // GRID, 2, S),
        ancestors,
        owner,
        weight_table,
        pole_slot,
    )
    column = column.transpose(1, 0, 2).reshape(BS, 1, 1, 2, S)
    return (
        column,
        diag.reshape(S // GRID, 1, 1, 2, S),
        density.reshape(S // GRID, 1, S),
        tile.reshape(1, 8, BS),
    )


def solution(mesh):
    grid = ("row", "col")
    in_specs = (
        P("pole", None, "row", "col"),
        P("pole", None, grid, None),
        P(grid, "pole", None, None, None),
        P(),
        P(grid, None),
        P(),
        P("pole"),
    )
    out_specs = (
        P(grid, "pole", None, None, None),
        P(grid, "pole", None, None, None),
        P(grid, None, None),
        P(("pole", "row", "col"), None, None),
    )
    return jax.shard_map(body, mesh=mesh, in_specs=in_specs, out_specs=out_specs, check_vma=False)
```

time: 241 us -> 83.6 us (0.35)
  waiting for transfers between devices: 117 us -> 0 us
  Pallas kernels: 0 us -> 73 us
  local copies, waits for them, and re-layouts: 42.6 us -> 8.48 us
  other arithmetic: 24.9 us -> 0 us
  starting transfers between devices: 23.6 us -> 0 us
  between operations: 15 us -> 1.29 us
  matrix products: 9.52 us -> 0 us
  blocking collectives: 7.7 us -> 0 us
    pallas_call x0 -> x1, Pallas kernels: none -> 73 us  [body(): pl.pallas_call(kernel, name='supernode', out_shape=(jax.ShapeDtypeStruct(...]
    all_to_all x4 -> x0, waiting for transfers between devices: 71.8 us -> none  [the longest x1 29.1 us: body(): lax.all_to_all(inverse, COL, split_axis=2, concat_axis=3, tiled=True)]
    all_gather x2 -> x0, waiting for transfers between devices: 44.9 us -> none  [all_blocks(): blocks = lax.all_gather(blocks, axes[k])]
    all_to_all x4 -> x0, starting transfers between devices: 23.5 us -> none  [the longest x1 7.96 us: body(): lax.all_to_all(outgoing, POLE_ROW_COL, split_axis=0, concat_axis=0, tiled...]
    another operation x3 -> x0, local copies, waits for them, and re-layouts: 18.4 us -> none
    concatenate x1 -> x0, other arithmetic: 9.67 us -> none  [body(): jnp.concatenate([-compact[:, :, :, :, 1:, :], compact[:, :, :, :, :1, :]]...]
    dot_general x7 -> x0, matrix products: 9.52 us -> none  [the longest x1 4.88 us: body(): jnp.einsum('kjn,pknbcs->jbpkcs', pick_rows, compact, preferred_element_ty...]
    neg x2 -> x0, other arithmetic: 9.35 us -> none  [the longest x1 9.33 us: body(): -compact[:, :, :, :, 1:, :]]
  transfers between devices with their start and end apart: 6 -> 0, of which waited for: 6 -> 0; matrix products, arithmetic and copies ran while one was open for 10% -> 0% of each run, Pallas kernels for 0% -> 0%
where the time goes in v1:
time: 83.6 us; the launch traced here: 82.8 us
  Pallas kernels  73 us (87%)
  local copies, waits for them, and re-layouts  8.48 us (10%)
  between operations  1.29 us (2%)
    pallas_call x1, Pallas kernels, body(): pl.pallas_call(kernel, name='supernode', out_shape=(jax.ShapeDtypeStruct(...  73 us
    unnamed x15, local copies, waits for them, and re-layouts  8.48 us

profile of v1, /device:TPU:1, one launch (start us, length us, event | category | flops | bytes accessed | tf_op | source)
XLA Modules:
  0.0 82.8 jit_solution(15478863156149410162)
XLA Ops:
  1.3 0.7 copy.11.owner
  2.0 0.0 copy-start
  2.0 1.6 %copy-done = bf16[1,2,1024,512]{3,2,1,0:T(8,128)(2,1)S(1)} copy-done((bf16[1,2,1024,512]{3,2,1,0:T(8,128)(2,1)S(1)}, bf16[1,2,1024,512]{3,2,1,0:T(8,128)(2,1)}, u32[]{:S(2)}) %copy-start) | copy-done | bytes 2097176
  3.6 0.0 copy-start.1
  3.6 0.9 %copy-done.1 = bf16[1,1,64,1024]{3,2,1,0:T(8,128)(2,1)S(1)} copy-done((bf16[1,1,64,1024]{3,2,1,0:T(8,128)(2,1)S(1)}, bf16[1,1,64,1024]{3,2,1,0:T(8,128)(2,1)}, u32[]{:S(2)}) %copy-start.1) | copy-done | bytes 131096
  4.5 0.0 copy-start.2
  4.5 0.8 %copy-done.2 = f32[16,1,1,2,512]{4,3,2,1,0:T(2,128)S(1)} copy-done((f32[16,1,1,2,512]{4,3,2,1,0:T(2,128)S(1)}, f32[16,1,1,2,512]{4,3,2,1,0:T(2,128)}, u32[]{:S(2)}) %copy-start.2) | copy-done | bytes 65560
  5.4 0.0 copy-start.3
  5.4 0.7 copy-done.3
  6.0 0.0 copy-start.4
  6.0 0.7 copy-done.4
  6.7 73.0 %supernode.1 = (f32[2,128,512]{2,1,0:T(8,128)S(1)}, f32[16,2,512]{2,1,0:T(2,128)S(1)}, f32[16,512]{1,0:T(8,128)S(1)}, f32[8,128]{1,0:T(8,128)S(1)}) custom-call(bf16[2,1024,512]{2,1,0:T(8,128)(2,1)S(1)} %bitcast.11, bf16[64,1024]{1,0:T(8,128)(2,1)S(1)} %bitcast.13, f32[16,2,512]{2,1,0:T(2,128)S(1)} %bitcast.15, s32[1,16]{1,0:T(1,128)S(1)} %copy-done.4, ...), custom_call_target="tpu_custom_call" | custom-call | tf_op jit(solution)/shard_map/supernode/pallas_call | solution.py:357
  79.7 1.2 %copy.12 = f32[128,1,1,2,512]{4,3,2,1,0:T(2,128)} copy(f32[128,1,1,2,512]{4,0,3,2,1:T(8,128)S(1)} %bitcast.12) | data formatting | bytes 1048576
  80.9 0.6 copy.14
  81.6 0.6 copy.18
  82.2 0.6 copy.19
Async XLA Ops:
  2.0 1.6 %copy-start = (bf16[1,2,1024,512]{3,2,1,0:T(8,128)(2,1)S(1)}, bf16[1,2,1024,512]{3,2,1,0:T(8,128)(2,1)}, u32[]{:S(2)}) copy-start(bf16[1,2,1024,512]{3,2,1,0:T(8,128)(2,1)} %param.7) | copy-start | bytes 6291460
  3.6 0.9 %copy-start.1 = (bf16[1,1,64,1024]{3,2,1,0:T(8,128)(2,1)S(1)}, bf16[1,1,64,1024]{3,2,1,0:T(8,128)(2,1)}, u32[]{:S(2)}) copy-start(bf16[1,1,64,1024]{3,2,1,0:T(8,128)(2,1)} %param.8) | copy-start | bytes 393220
  4.5 0.8 %copy-start.2 = (f32[16,1,1,2,512]{4,3,2,1,0:T(2,128)S(1)}, f32[16,1,1,2,512]{4,3,2,1,0:T(2,128)}, u32[]{:S(2)}) copy-start(f32[16,1,1,2,512]{4,3,2,1,0:T(2,128)} %param.9) | copy-start | bytes 196612
  5.4 0.7 copy-start.3
  6.0 0.7 copy-start.4

commit v2 on v1

--- a/solution.py
+++ b/solution.py
@@ -23,10 +23,10 @@
 def kernel(
     inverse,
     factor,
-    dinv,
-    ancestors,
-    owner,
-    table,
+    dinv_in,
+    ancestors_in,
+    owner_in,
+    table_in,
     slot,
     column_out,
     diag_out,
@@ -36,7 +36,10 @@
     gbuf,
     abuf,
     acc,
-    col_buf,
+    dinv,
+    owner,
+    ancestors,
+    table,
     ysend,
     yrecv,
     dsend,
@@ -65,7 +68,6 @@
     p_recv,
     q_send,
     q_recv,
-    out_sem,
 ):
     pole, row, col = lax.axis_index("pole"), lax.axis_index("row"), lax.axis_index("col")
     side, depth = col // 4, col % 4
@@ -103,6 +105,20 @@
 
     for k in range(4):
         pltpu.make_async_copy(piece(col, k), gbuf.at[col * 4 + k], local_sem.at[1]).start()
+
+    small = [
+        pltpu.make_async_copy(source, target, local_sem.at[2 + n])
+        for n, (source, target) in enumerate(
+            (
+                (owner_in, owner),
+                (ancestors_in, ancestors),
+                (table_in, table),
+                (dinv_in, dinv),
+            )
+        )
+    ]
+    for copy in small:
+        copy.start()
 
     barrier = pltpu.get_barrier_semaphore()
     others = [(ds, dz) for ds in (0, 1) for dz in (0, 1, 3, 2) if (ds, dz) != (0, 0)]
@@ -204,7 +220,12 @@
     lane = lax.broadcasted_iota(jnp.int32, (64, 512), 1)
     owner_index = lax.broadcasted_iota(jnp.int32, (64, 512), 0)
     mine = ((lane & 127) >> 3) * 4 + (lane >> 7)
-    target = owner[...]
+    for copy in small:
+        copy.wait()
+    across = lax.broadcasted_iota(jnp.int32, (64, 64), 1)
+    down = lax.broadcasted_iota(jnp.int32, (64, 64), 0)
+    target = jnp.where(across == down, owner[...].astype(F32), 0.0)
+    target = jnp.sum(target, axis=1, keepdims=True).astype(jnp.int32)
     target = ((target & 31) * 32 + (target >> 5) * 8).astype(F32)
     spread = jnp.where(mine == owner_index, target, 0.0)
     key = jnp.sum(spread, axis=0, keepdims=True) + (lane[:1] & 7).astype(F32)
@@ -242,10 +263,6 @@
     keep = lax.broadcast_in_dim(chosen, (BS, S), ()) > 0
     real = jnp.where(keep, real, 0.0)
     imag = jnp.where(keep, imag, 0.0)
-    col_buf[0] = -real
-    col_buf[1] = -imag
-    column_copy = pltpu.make_async_copy(col_buf, column_out, out_sem)
-    column_copy.start()
     for q in range(4):
         lanes = slice(q * BS, (q + 1) * BS)
         ysend[q] = jnp.concatenate([real[:, lanes], imag[:, lanes]], axis=1).astype(BF)
@@ -275,6 +292,8 @@
 
     lax.fori_loop(1, GRID, send_tiles, 0)
     trecv[me] = tsend[me]
+    column_out[:, 0, :] = -real
+    column_out[:, 1, :] = -imag
 
     for k in (1, 3, 2):
         r = up(k)
@@ -338,7 +357,7 @@
     for k in range(1, POLES):
         p = (pole + k) % POLES
         remote(qsend, qrecv.at[p], q_send.at[0], q_recv.at[p], (pole, row, col)).wait_recv()
-    density_out[...] = jnp.sum(qrecv[...], axis=0)
+    density_out[:, 0, :] = jnp.sum(qrecv[...], axis=0)
 
     arrived.wait_send()
     landed.wait_send()
@@ -346,31 +365,41 @@
         copy.wait_send()
     for n in range(COLS - 1):
         strip(col, n).wait_send()
-    column_copy.wait()
+
+
+def hand_out(*refs):
+    done = refs[8]
+    copies = [pltpu.make_async_copy(refs[k], refs[4 + k], done.at[k]) for k in range(4)]
+    for copy in copies:
+        copy.start()
+    for copy in copies:
+        copy.wait()
 
 
 def body(inverse, factor, dinv, ancestors, owner, weight_table, pole_slot):
     vmem = pl.BlockSpec(memory_space=pltpu.VMEM)
-    smem = pl.BlockSpec(memory_space=pltpu.SMEM)
     hbm = pl.BlockSpec(memory_space=pl.ANY)
     dma = pltpu.SemaphoreType.DMA
     column, diag, density, tile = pl.pallas_call(
         kernel,
         name="supernode",
         out_shape=(
-            jax.ShapeDtypeStruct((2, BS, S), F32),
-            jax.ShapeDtypeStruct((S // GRID, 2, S), F32),
-            jax.ShapeDtypeStruct((S // GRID, S), F32),
-            jax.ShapeDtypeStruct((8, BS), F32),
+            pltpu.VMEM((BS, 2, S), F32),
+            pltpu.VMEM((S // GRID, 2, S), F32),
+            pltpu.VMEM((S // GRID, 1, S), F32),
+            pltpu.VMEM((8, BS), F32),
         ),
-        in_specs=[hbm, hbm, vmem, smem, vmem, smem, smem],
-        out_specs=(hbm, vmem, vmem, vmem),
+        in_specs=[pl.BlockSpec(memory_space=pltpu.HBM)] * 6 + [pl.BlockSpec(memory_space=pltpu.SMEM)],
+        out_specs=(vmem,) * 4,
         scratch_shapes=[
             pltpu.VMEM((NSEL, BS, 2 * S), BF),
             pltpu.VMEM((COLS * 4, 2, BS, BS), BF),
             pltpu.VMEM((4, 2 * BS, 4 * BS), BF),
             pltpu.VMEM((2 * BS, 2 * S), F32),
-            pltpu.VMEM((2, BS, S), F32),
+            pltpu.VMEM((S // GRID, 2, S), F32),
+            pltpu.VMEM((1, 64), jnp.int32),
+            pltpu.SMEM((1, NSEL), jnp.int32),
+            pltpu.SMEM((2, NWEIGHT), F32),
             pltpu.VMEM((4, BS, 2 * BS), BF),
             pltpu.VMEM((4, BS, 2 * BS), BF),
             pltpu.VMEM((GRID, S // GRID, 2 * BS), BF),
@@ -382,7 +411,7 @@
             pltpu.VMEM((POLES, 8, BS), F32),
             pltpu.VMEM((S // GRID, S), F32),
             pltpu.VMEM((POLES, S // GRID, S), F32),
-            dma((2,)),
+            dma((7,)),
             dma((24,)),
             dma((GRID,)),
             dma((16,)),
@@ -399,25 +428,37 @@
             dma((POLES,)),
             dma((POLES,)),
             dma((POLES,)),
-            dma,
         ],
         compiler_params=pltpu.CompilerParams(
-            collective_id=0, has_side_effects=True, vmem_limit_bytes=48 << 20
+            collective_id=0, has_side_effects=True, vmem_limit_bytes=56 << 20
         ),
     )(
-        inverse.reshape(2, 1024, 512),
-        factor.reshape(LROWS, 2 * S),
-        dinv.reshape(S // GRID, 2, S),
-        ancestors,
-        owner,
-        weight_table,
+        *(
+            pltpu.with_memory_space_constraint(x, pltpu.HBM)
+            for x in (
+                inverse.reshape(2, 1024, 512),
+                factor.reshape(LROWS, 2 * S),
+                dinv.reshape(S // GRID, 2, S),
+                ancestors,
+                owner.reshape(1, 64),
+                weight_table,
+            )
+        ),
         pole_slot,
     )
-    column = column.transpose(1, 0, 2).reshape(BS, 1, 1, 2, S)
+    column, diag, density, tile = pl.pallas_call(
+        hand_out,
+        name="hand_out",
+        out_shape=tuple(jax.ShapeDtypeStruct(x.shape, F32) for x in (column, diag, density, tile)),
+        in_specs=[vmem] * 4,
+        out_specs=(hbm,) * 4,
+        scratch_shapes=[dma((4,))],
+        compiler_params=pltpu.CompilerParams(vmem_limit_bytes=1 << 20),
+    )(column, diag, density, tile)
     return (
-        column,
+        column.reshape(BS, 1, 1, 2, S),
         diag.reshape(S // GRID, 1, 1, 2, S),
-        density.reshape(S // GRID, 1, S),
+        density,
         tile.reshape(1, 8, BS),
     )
 

time: 83.6 us -> 74.4 us (0.89)
  local copies, waits for them, and re-layouts: 8.48 us -> 0 us
    unnamed x15 -> x0, local copies, waits for them, and re-layouts: 8.48 us -> none
    pallas_call x1 -> x2, Pallas kernels: 73 us -> 72.4 us  [the longest x1 71.5 us: body(): pl.pallas_call(kernel, name='supernode', out_shape=(pltpu.VMEM((BS, 2, S)...]
where the time goes in v2:
time: 74.4 us; the launch traced here: 73.6 us
  Pallas kernels  72.4 us (97%)
  between operations  1.29 us (2%)
    pallas_call x1, Pallas kernels, body(): pl.pallas_call(kernel, name='supernode', out_shape=(pltpu.VMEM((BS, 2, S)...  71.5 us

profile of v2, /device:TPU:1, one launch (start us, length us, event | category | flops | bytes accessed | tf_op | source)
XLA Modules:
  0.0 73.6 jit_solution(13078695569481484129)
XLA Ops:
  1.3 71.5 %supernode.1 = (f32[128,2,512]{2,1,0:T(2,128)S(1)}, f32[16,2,512]{2,1,0:T(2,128)S(1)}, f32[16,1,512]{2,1,0:T(1,128)S(1)}, f32[8,128]{1,0:T(8,128)S(1)}) custom-call(bf16[2,1024,512]{2,1,0:T(8,128)(2,1)} %bitcast.11, bf16[64,1024]{1,0:T(8,128)(2,1)} %bitcast.12, f32[16,2,512]{2,1,0:T(2,128)} %bitcast.13, s32[1,16]{1,0:T(1,128)} %ancestors_in.1, ...), custom_call_target="tpu_custom_call" | custom-call | tf_op jit(solution)/shard_map/supernode/pallas_call | solution.py:383
  72.8 0.8 %hand_out.1 = (f32[128,2,512]{2,1,0:T(2,128)}, f32[16,2,512]{2,1,0:T(2,128)}, f32[16,1,512]{2,1,0:T(1,128)}, f32[8,128]{1,0:T(8,128)}) custom-call(f32[128,2,512]{2,1,0:T(2,128)S(1)} %get-tuple-element.12.refs_0_, f32[16,2,512]{2,1,0:T(2,128)S(1)} %get-tuple-element.13.refs_1_, f32[16,1,512]{2,1,0:T(1,128)S(1)} %get-tuple-element.14.refs_2_, ...), custom_call_target="tpu_custom_call" | custom-call | tf_op jit(solution)/shard_map/hand_out/pallas_call | solution.py:449

commit v3 on v2

v3 whole, which is shorter than its diff:
```python
import jax
import jax.numpy as jnp
from jax import lax
from jax.experimental import pallas as pl
from jax.experimental.pallas import tpu as pltpu
from jax.sharding import PartitionSpec as P

S = 512
BS = 128
NSEL = 16
NWEIGHT = 16
ROWS = 4
COLS = 8
POLES = 4
GRID = ROWS * COLS
LROWS = NSEL * BS // GRID
HALF = LROWS // 2
MESH = pl.DeviceIdType.MESH
BF = jnp.bfloat16
F32 = jnp.float32


def kernel(
    inverse,
    factor,
    dinv_in,
    ancestors_in,
    owner_in,
    table_in,
    slot,
    column_out,
    diag_out,
    density_out,
    tile_out,
    lbuf,
    first_strips,
    second_strips,
    abuf,
    left,
    column_send,
    dinv,
    owner,
    ancestors,
    table,
    ysend,
    yrecv,
    dsend,
    drecv,
    pick,
    tsend,
    trecv,
    psend,
    precv,
    qsend,
    qrecv,
    local_sem,
    l_send,
    l_recv,
    h_send,
    h_recv,
    g_send,
    g_recv,
    o_send,
    o_recv,
    c_send,
    c_recv,
    y_send,
    y_recv,
    d_send,
    d_recv,
    t_send,
    t_recv,
    p_send,
    p_recv,
    q_send,
    q_recv,
):
    pole, row, col = lax.axis_index("pole"), lax.axis_index("row"), lax.axis_index("col")
    side, depth = col // 4, col % 4
    me = row * COLS + col
    works = pole % 2
    active = side == works
    facing = (1 - side) * 4 + depth
    source = row * 4 + depth
    turns = (1 - works, works)
    strips = (first_strips, second_strips)

    def at_depth(s, dz):
        return s * 4 + (depth + dz) % 4

    def up(k):
        return (row + k) % ROWS

    def remote(src, dst, send, recv, to):
        return pltpu.make_async_remote_copy(
            src_ref=src,
            dst_ref=dst,
            send_sem=send,
            recv_sem=recv,
            device_id=to,
            device_id_type=MESH,
        )

    here = (pole, row, col)

    def sent(ref, send):
        remote(ref, ref, send, q_recv.at[0], here).wait_send()

    def came(ref, recv):
        remote(ref, ref, q_send.at[0], recv, here).wait_recv()

    own_factor = pltpu.make_async_copy(
        factor, lbuf.at[me // 2, pl.ds((me % 2) * LROWS, LROWS)], local_sem.at[0]
    )
    own_factor.start()
    small = [
        pltpu.make_async_copy(source, target, local_sem.at[2 + n])
        for n, (source, target) in enumerate(
            (
                (owner_in, owner.at[side]),
                (ancestors_in, ancestors),
                (table_in, table),
                (dinv_in, dinv),
            )
        )
    ]
    for copy in small:
        copy.start()

    def piece(rb, z, k):
        return inverse.at[:, pl.ds((rb * 4 + z) * BS, BS), pl.ds(k * BS, BS)]

    @pl.when(active)
    def _():
        for j, rb in enumerate(turns):
            for k in range(4):
                pltpu.make_async_copy(
                    piece(rb, depth, k), strips[j].at[col * 4 + k], local_sem.at[6 * j + 1]
                ).start()

    barrier = pltpu.get_barrier_semaphore()
    others = [(ds, dz) for ds in (0, 1) for dz in (0, 1, 3, 2) if (ds, dz) != (0, 0)]
    for ds, dz in others:
        c = ((side + ds) % 2) * 4 + (depth + dz) % 4
        pl.semaphore_signal(barrier, inc=1, device_id=(pole, row, c), device_id_type=MESH)
    for k in (1, 3, 2):
        pl.semaphore_signal(barrier, inc=1, device_id=(pole, up(k), col), device_id_type=MESH)
    for k in range(1, POLES):
        pl.semaphore_signal(
            barrier, inc=1, device_id=((pole + k) % POLES, row, col), device_id_type=MESH
        )
    pl.semaphore_wait(barrier, len(others) + ROWS - 1 + POLES - 1)
    own_factor.wait()
    for copy in small:
        copy.wait()

    def block(r, c):
        return lbuf.at[r * 4 + c // 2, pl.ds((c % 2) * LROWS, LROWS)]

    def half(r, c, part):
        return lbuf.at[r * 4 + c // 2, pl.ds((c % 2) * LROWS + part * HALF, HALF)]

    def send_strip(n, j, z):
        for k in range(4):
            remote(
                piece(turns[j], z, k),
                strips[j].at[col * 4 + k],
                g_send.at[n],
                g_recv.at[j, col],
                (pole, row, works * 4 + z),
            ).start()

    @pl.when(jnp.logical_not(active))
    def _():
        remote(
            block(row, col), block(row, col), l_send.at[0], l_recv.at[me], (pole, row, facing)
        ).start()
        remote(owner.at[side], owner.at[side], o_send, o_recv, (pole, row, facing)).start()
        n = 0
        for j in range(2):
            for dz in (2, 1, 3, 0):
                send_strip(n, j, (depth + dz) % 4)
                n += 1

    weight_real = table[0, slot[0]]
    weight_imag = table[1, slot[0]]

    def to_position(k):
        to = (me + k) % GRID
        return to, (pole, to // COLS, to % COLS)

    @pl.when(active)
    def _():
        count = [0]

        def send_block(r, c, to):
            k = count[0]
            count[0] += 1
            remote(
                block(r, c), block(r, c), l_send.at[k], l_recv.at[r * COLS + c], to
            ).start()

        def send_half(r, c, part, k, to):
            remote(
                half(r, c, part), half(r, c, part), h_send.at[k], h_recv.at[part, c], to
            ).start()

        def wait_block(r, c):
            came(block(r, c), l_recv.at[r * COLS + c])

        def along_rows(c):
            send_block(row, c, (pole, up(1), col))
            send_block(row, c, (pole, up(3), col))

        for c in (col, facing):
            if c is facing:
                wait_block(row, facing)
            for dz in (1, 3, 2):
                send_block(row, c, (pole, row, at_depth(side, dz)))
            along_rows(c)
        n = 0
        for j in range(2):
            for dz in (2, 1, 3):
                send_strip(n, j, (depth + dz) % 4)
                n += 1
        order = [col, facing]
        for dz in (1, 3, 2):
            order += [at_depth(side, dz), at_depth(1 - side, dz)]
        for c in order[2:]:
            wait_block(row, c)
            along_rows(c)
        for k, c in enumerate(order):
            wait_block(up(3), c)
            send_half(up(3), c, 0, 2 * k, (pole, up(1), col))
            wait_block(up(1), c)
            send_half(up(1), c, 1, 2 * k + 1, (pole, up(3), col))

        came(owner.at[0], o_recv)
        lane = lax.broadcasted_iota(jnp.int32, (64, 512), 1)
        owner_index = lax.broadcasted_iota(jnp.int32, (64, 512), 0)
        named = ((lane & 127) >> 3) * 4 + (lane >> 7)
        across = lax.broadcasted_iota(jnp.int32, (64, 64), 1)
        down = lax.broadcasted_iota(jnp.int32, (64, 64), 0)
        position = lax.broadcasted_iota(jnp.int32, (1024, 512), 0).astype(F32)
        for s in range(2):
            target = jnp.where(across == down, owner[s].astype(F32), 0.0)
            target = jnp.sum(target, axis=1, keepdims=True).astype(jnp.int32)
            target = ((target & 31) * 32 + (target >> 5) * 8).astype(F32)
            spread = jnp.where(named == owner_index, target, 0.0)
            key = jnp.sum(spread, axis=0, keepdims=True) + (lane[:1] & 7).astype(F32)
            pick[:, s * 512 : (s + 1) * 512] = jnp.where(position == key, 1.0, 0.0).astype(BF)

        for c in order:
            came(half(up(2), c, 0), h_recv.at[0, c])
            came(half(up(2), c, 1), h_recv.at[1, c])
        for r in range(4):
            for s in range(2):
                b = r * COLS + s * 4 + depth
                before = jnp.int32(0)
                for i in range(NSEL):
                    before += jnp.where(ancestors[0, i] < b, 1, 0)
                before = jnp.minimum(before, NSEL - 1)
                at = (2 * r + s) * BS
                left[:, at : at + BS] = lbuf[before].T

        shares = [None, None]
        columns = []
        for j, rb in enumerate(turns):
            for s in (0, 1):
                for dz in (1, 3, 2, 0):
                    c = at_depth(s, dz)

                    @pl.when(c != col)
                    def _():
                        came(strips[j].at[pl.ds(0, 4)], g_recv.at[j, c])

            own = strips[j].at[pl.ds(col * 4, 4)]
            pltpu.make_async_copy(own, own, local_sem.at[6 * j + 1]).wait()
            for i in range(NSEL):
                for part in range(2):
                    abuf[part * BS : (part + 1) * BS, i * BS : (i + 1) * BS] = strips[j][
                        ancestors[0, i], part
                    ]
            acc = jnp.dot(
                abuf[...], lbuf[...].reshape(NSEL * BS, 2 * S), preferred_element_type=F32
            )
            real = acc[:BS, :S] - acc[BS:, S:]
            imag = acc[:BS, S:] + acc[BS:, :S]
            chosen = jnp.int32(0)
            for i in range(NSEL):
                chosen += jnp.where(ancestors[0, i] == row * COLS + rb * 4 + depth, 1, 0)
            keep = lax.broadcast_in_dim(chosen, (BS, S), ()) > 0
            real = jnp.where(keep, real, 0.0)
            imag = jnp.where(keep, imag, 0.0)
            for q in range(4):
                lanes = slice(q * BS, (q + 1) * BS)
                ysend[q, rb] = jnp.concatenate([real[:, lanes], imag[:, lanes]], axis=1).astype(BF)
            for k in (2, 1, 3):
                r = up(k)
                remote(
                    ysend.at[r, rb],
                    yrecv.at[row, rb],
                    y_send.at[j, k],
                    y_recv.at[row, rb],
                    (pole, r, col),
                ).start()
            yrecv[row, rb] = ysend[row, rb]
            target = (column_send, column_out)[j]
            target[:, 0, :] = -real
            target[:, 1, :] = -imag
            if j == 0:
                remote(column_send, column_out, c_send, c_recv, (pole, row, facing)).start()
            share = -(weight_real * imag + weight_imag * real)
            columns.append(
                jnp.concatenate([share[:, q * BS : (q + 1) * BS] for q in range(4)], axis=0)
            )
        first = lax.broadcast_in_dim(works, columns[0].shape, ()) == 1
        share = jnp.concatenate(
            [
                jnp.where(first, columns[0], columns[1]),
                jnp.where(first, columns[1], columns[0]),
            ],
            axis=0,
        )
        high = share.astype(BF)
        low = (share - high.astype(F32)).astype(BF)
        tiles = jnp.dot(
            pick[...], jnp.concatenate([high, low], axis=1), preferred_element_type=F32
        )
        tiles = tiles[:, :BS] + tiles[:, BS:]
        tsend[...] = tiles.astype(BF).reshape(GRID, 32, BS)

        def send_tiles(k, carry):
            to, device = to_position(k)
            remote(tsend.at[to], trecv.at[source], t_send, t_recv, device).start()
            return carry

        lax.fori_loop(1, GRID, send_tiles, 0)
        trecv[source] = tsend[me]

        for k in (1, 3, 2):
            for rb in range(2):
                came(ysend.at[0, 0], y_recv.at[up(k), rb])
        mixed = jnp.dot(
            left[...], yrecv[...].reshape(8 * BS, 2 * BS), preferred_element_type=F32
        )
        diag_real = mixed[:S, :BS] - mixed[S:, BS:]
        diag_imag = mixed[:S, BS:] + mixed[S:, :BS]
        dsend[...] = (
            jnp.concatenate([diag_real, diag_imag], axis=1)
            .astype(BF)
            .reshape(GRID, S // GRID, 2 * BS)
        )

        def send_diag(k, carry):
            to, device = to_position(k)
            remote(dsend.at[to], drecv.at[source], d_send, d_recv, device).start()
            return carry

        lax.fori_loop(1, GRID, send_diag, 0)
        drecv[source] = dsend[me]

    def arrivals(ref, recv):
        @pl.when(active)
        def _():
            came(ref.at[pl.ds(0, GRID // 2 - 1)], recv)

        @pl.when(jnp.logical_not(active))
        def _():
            came(ref, recv)

    arrivals(trecv, t_recv)
    total = jnp.sum(trecv[...].astype(F32), axis=0)
    psend[...] = total.reshape(POLES, 8, BS)
    for k in range(1, POLES):
        p = (pole + k) % POLES
        remote(psend.at[p], precv.at[pole], p_send.at[k], p_recv.at[pole], (p, row, col)).start()
    precv[pole] = psend[pole]

    arrivals(drecv, d_recv)
    dreal, dimag = [], []
    for q in range(4):
        quarter = jnp.sum(drecv[q * 4 : (q + 1) * 4].astype(F32), axis=0)
        dreal.append(quarter[:, :BS])
        dimag.append(quarter[:, BS:])
    dreal = jnp.concatenate(dreal, axis=1) + dinv[:, 0, :]
    dimag = jnp.concatenate(dimag, axis=1) + dinv[:, 1, :]
    qsend[...] = weight_real * dimag + weight_imag * dreal
    for k in range(1, POLES):
        p = (pole + k) % POLES
        remote(qsend, qrecv.at[pole], q_send.at[k], q_recv.at[pole], (p, row, col)).start()
    qrecv[pole] = qsend[...]
    diag_out[:, 0, :] = dreal
    diag_out[:, 1, :] = dimag
    for k in range(1, POLES):
        p = (pole + k) % POLES
        came(psend.at[0], p_recv.at[p])
    tile_out[...] = jnp.sum(precv[...], axis=0)

    @pl.when(jnp.logical_not(active))
    def _():
        sent(lbuf.at[0, pl.ds(0, LROWS)], l_send.at[0])
        sent(owner.at[0], o_send)
        for n in range(8):
            sent(first_strips.at[pl.ds(0, 4)], g_send.at[n])
        came(column_out, c_recv)

    @pl.when(active)
    def _():
        for n in range(22):
            sent(lbuf.at[0, pl.ds(0, LROWS)], l_send.at[n])
        for n in range(16):
            sent(lbuf.at[0, pl.ds(0, HALF)], h_send.at[n])
        for n in range(6):
            sent(first_strips.at[pl.ds(0, 4)], g_send.at[n])
        for j in range(2):
            for k in (1, 2, 3):
                sent(ysend.at[0, 0], y_send.at[j, k])
        sent(column_send, c_send)
        sent(tsend.at[pl.ds(0, GRID - 1)], t_send)
        sent(dsend.at[pl.ds(0, GRID - 1)], d_send)

    for k in range(1, POLES):
        sent(psend.at[0], p_send.at[k])
        sent(qsend, q_send.at[k])
    for k in range(1, POLES):
        p = (pole + k) % POLES
        came(qsend, q_recv.at[p])
    density_out[:, 0, :] = jnp.sum(qrecv[...], axis=0)


def hand_out(*refs):
    done = refs[8]
    copies = [pltpu.make_async_copy(refs[k], refs[4 + k], done.at[k]) for k in range(4)]
    for copy in copies:
        copy.start()
    for copy in copies:
        copy.wait()


def body(inverse, factor, dinv, ancestors, owner, weight_table, pole_slot):
    vmem = pl.BlockSpec(memory_space=pltpu.VMEM)
    hbm = pl.BlockSpec(memory_space=pl.ANY)
    dma = pltpu.SemaphoreType.DMA
    column, diag, density, tile = pl.pallas_call(
        kernel,
        name="supernode",
        out_shape=(
            pltpu.VMEM((BS, 2, S), F32),
            pltpu.VMEM((S // GRID, 2, S), F32),
            pltpu.VMEM((S // GRID, 1, S), F32),
            pltpu.VMEM((8, BS), F32),
        ),
        in_specs=[pl.BlockSpec(memory_space=pltpu.HBM)] * 6 + [pl.BlockSpec(memory_space=pltpu.SMEM)],
        out_specs=(vmem,) * 4,
        scratch_shapes=[
            pltpu.VMEM((NSEL, BS, 2 * S), BF),
            pltpu.VMEM((COLS * 4, 2, BS, BS), BF),
            pltpu.VMEM((COLS * 4, 2, BS, BS), BF),
            pltpu.VMEM((2 * BS, NSEL * BS), BF),
            pltpu.VMEM((2 * S, 8 * BS), BF),
            pltpu.VMEM((BS, 2, S), F32),
            pltpu.VMEM((S // GRID, 2, S), F32),
            pltpu.VMEM((2, 1, 64), jnp.int32),
            pltpu.SMEM((1, NSEL), jnp.int32),
            pltpu.SMEM((2, NWEIGHT), F32),
            pltpu.VMEM((4, 2, BS, 2 * BS), BF),
            pltpu.VMEM((4, 2, BS, 2 * BS), BF),
            pltpu.VMEM((GRID, S // GRID, 2 * BS), BF),
            pltpu.VMEM((GRID // 2, S // GRID, 2 * BS), BF),
            pltpu.VMEM((1024, 1024), BF),
            pltpu.VMEM((GRID, 32, BS), BF),
            pltpu.VMEM((GRID // 2, 32, BS), BF),
            pltpu.VMEM((POLES, 8, BS), F32),
            pltpu.VMEM((POLES, 8, BS), F32),
            pltpu.VMEM((S // GRID, S), F32),
            pltpu.VMEM((POLES, S // GRID, S), F32),
            dma((8,)),
            dma((22,)),
            dma((GRID,)),
            dma((16,)),
            dma((2, COLS)),
            dma((8,)),
            dma((2, COLS)),
            dma,
            dma,
            dma,
            dma,
            dma((2, 4)),
            dma((4, 2)),
            dma,
            dma,
            dma,
            dma,
            dma((POLES,)),
            dma((POLES,)),
            dma((POLES,)),
            dma((POLES,)),
        ],
        compiler_params=pltpu.CompilerParams(
            collective_id=0, has_side_effects=True, vmem_limit_bytes=56 << 20
        ),
    )(
        *(
            pltpu.with_memory_space_constraint(x, pltpu.HBM)
            for x in (
                inverse.reshape(2, 1024, 512),
                factor.reshape(LROWS, 2 * S),
                dinv.reshape(S // GRID, 2, S),
                ancestors,
                owner.reshape(1, 64),
                weight_table,
            )
        ),
        pole_slot,
    )
    column, diag, density, tile = pl.pallas_call(
        hand_out,
        name="hand_out",
        out_shape=tuple(jax.ShapeDtypeStruct(x.shape, F32) for x in (column, diag, density, tile)),
        in_specs=[vmem] * 4,
        out_specs=(hbm,) * 4,
        scratch_shapes=[dma((4,))],
        compiler_params=pltpu.CompilerParams(vmem_limit_bytes=1 << 20),
    )(column, diag, density, tile)
    return (
        column.reshape(BS, 1, 1, 2, S),
        diag.reshape(S // GRID, 1, 1, 2, S),
        density,
        tile.reshape(1, 8, BS),
    )


def solution(mesh):
    grid = ("row", "col")
    in_specs = (
        P("pole", None, "row", "col"),
        P("pole", None, grid, None),
        P(grid, "pole", None, None, None),
        P(),
        P(grid, None),
        P(),
        P("pole"),
    )
    out_specs = (
        P(grid, "pole", None, None, None),
        P(grid, "pole", None, None, None),
        P(grid, None, None),
        P(("pole", "row", "col"), None, None),
    )
    return jax.shard_map(body, mesh=mesh, in_specs=in_specs, out_specs=out_specs, check_vma=False)
```

time: 74.4 us -> 64 us (0.86)
  the two profiles are of different devices: /device:TPU:1 before, /device:TPU:7 now
where the time goes in v3:
time: 64 us; the launch traced here: 63.9 us
  Pallas kernels  62.6 us (98%)
  between operations  1.29 us (2%)
    pallas_call x1, Pallas kernels, body(): pl.pallas_call(kernel, name='supernode', out_shape=(pltpu.VMEM((BS, 2, S)...  61.8 us

profile of v3, /device:TPU:7, one launch (start us, length us, event | category | flops | bytes accessed | tf_op | source)
XLA Modules:
  0.0 63.9 jit_solution(6067100203886073406)
XLA Ops:
  1.3 61.8 %supernode.1 = (f32[128,2,512]{2,1,0:T(2,128)S(1)}, f32[16,2,512]{2,1,0:T(2,128)S(1)}, f32[16,1,512]{2,1,0:T(1,128)S(1)}, f32[8,128]{1,0:T(8,128)S(1)}) custom-call(bf16[2,1024,512]{2,1,0:T(8,128)(2,1)} %bitcast.11, bf16[64,1024]{1,0:T(8,128)(2,1)} %bitcast.12, f32[16,2,512]{2,1,0:T(2,128)} %bitcast.13, s32[1,16]{1,0:T(1,128)} %ancestors_in.1, ...), custom_call_target="tpu_custom_call" | custom-call | tf_op jit(solution)/shard_map/supernode/pallas_call | solution.py:445
  63.1 0.8 %hand_out.1 = (f32[128,2,512]{2,1,0:T(2,128)}, f32[16,2,512]{2,1,0:T(2,128)}, f32[16,1,512]{2,1,0:T(1,128)}, f32[8,128]{1,0:T(8,128)}) custom-call(f32[128,2,512]{2,1,0:T(2,128)S(1)} %get-tuple-element.12.refs_0_, f32[16,2,512]{2,1,0:T(2,128)S(1)} %get-tuple-element.13.refs_1_, f32[16,1,512]{2,1,0:T(1,128)S(1)} %get-tuple-element.14.refs_2_, ...), custom_call_target="tpu_custom_call" | custom-call | tf_op jit(solution)/shard_map/hand_out/pallas_call | solution.py:517

commit v4 on v3

--- a/solution.py
+++ b/solution.py
@@ -35,6 +35,7 @@
     lbuf,
     first_strips,
     second_strips,
+    relay,
     abuf,
     left,
     column_send,
@@ -60,6 +61,8 @@
     h_recv,
     g_send,
     g_recv,
+    r_send,
+    s_recv,
     o_send,
     o_recv,
     c_send,
@@ -176,11 +179,17 @@
             block(row, col), block(row, col), l_send.at[0], l_recv.at[me], (pole, row, facing)
         ).start()
         remote(owner.at[side], owner.at[side], o_send, o_recv, (pole, row, facing)).start()
-        n = 0
         for j in range(2):
-            for dz in (2, 1, 3, 0):
-                send_strip(n, j, (depth + dz) % 4)
-                n += 1
+            for i, dz in enumerate((1, 3, 2, 0)):
+                z = (depth + dz) % 4
+                for k in range(4):
+                    remote(
+                        piece(turns[j], z, k),
+                        relay.at[j, i, k] if dz else strips[j].at[col * 4 + k],
+                        g_send.at[4 * j + i],
+                        s_recv.at[j, i] if dz else g_recv.at[j, col],
+                        (pole, row, facing),
+                    ).start()
 
     weight_real = table[0, slot[0]]
     weight_imag = table[1, slot[0]]
@@ -212,28 +221,62 @@
             send_block(row, c, (pole, up(1), col))
             send_block(row, c, (pole, up(3), col))
 
-        for c in (col, facing):
-            if c is facing:
-                wait_block(row, facing)
+        def pass_on(c):
+            k = passed[0]
+            passed[0] += 2
+            wait_block(up(3), c)
+            send_half(up(3), c, 0, k, (pole, up(1), col))
+            wait_block(up(1), c)
+            send_half(up(1), c, 1, k + 1, (pole, up(3), col))
+
+        def in_plane(c):
             for dz in (1, 3, 2):
                 send_block(row, c, (pole, row, at_depth(side, dz)))
             along_rows(c)
-        n = 0
-        for j in range(2):
-            for dz in (2, 1, 3):
-                send_strip(n, j, (depth + dz) % 4)
-                n += 1
+
+        def arrived_in_plane(c):
+            wait_block(row, c)
+            along_rows(c)
+
+        def forward(j, i):
+            came(relay.at[j, i], s_recv.at[j, i])
+            remote(
+                relay.at[j, i],
+                strips[j].at[pl.ds(facing * 4, 4)],
+                r_send.at[j, i],
+                g_recv.at[j, facing],
+                (pole, row, at_depth(side, (1, 3, 2)[i])),
+            ).start()
+
+        def send_own(j, i):
+            send_strip(3 * j + i, j, (depth + (1, 3, 2)[i]) % 4)
+
+        passed = [0]
         order = [col, facing]
         for dz in (1, 3, 2):
             order += [at_depth(side, dz), at_depth(1 - side, dz)]
-        for c in order[2:]:
-            wait_block(row, c)
-            along_rows(c)
-        for k, c in enumerate(order):
-            wait_block(up(3), c)
-            send_half(up(3), c, 0, 2 * k, (pole, up(1), col))
-            wait_block(up(1), c)
-            send_half(up(1), c, 1, 2 * k + 1, (pole, up(3), col))
+        in_plane(col)
+        send_own(0, 0)
+        send_own(0, 1)
+        wait_block(row, facing)
+        in_plane(facing)
+        arrived_in_plane(order[2])
+        arrived_in_plane(order[4])
+        forward(0, 0)
+        forward(0, 1)
+        send_own(0, 2)
+        for k in (3, 5, 6, 7):
+            arrived_in_plane(order[k])
+        forward(0, 2)
+        send_own(1, 0)
+        send_own(1, 1)
+        for k in (0, 1, 2, 4):
+            pass_on(order[k])
+        forward(1, 0)
+        send_own(1, 2)
+        for k in (3, 5, 6, 7):
+            pass_on(order[k])
+        forward(1, 1)
 
         came(owner.at[0], o_recv)
         lane = lax.broadcasted_iota(jnp.int32, (64, 512), 1)
@@ -250,6 +293,7 @@
             key = jnp.sum(spread, axis=0, keepdims=True) + (lane[:1] & 7).astype(F32)
             pick[:, s * 512 : (s + 1) * 512] = jnp.where(position == key, 1.0, 0.0).astype(BF)
 
+        forward(1, 2)
         for c in order:
             came(half(up(2), c, 0), h_recv.at[0, c])
             came(half(up(2), c, 1), h_recv.at[1, c])
@@ -414,6 +458,8 @@
         for n in range(6):
             sent(first_strips.at[pl.ds(0, 4)], g_send.at[n])
         for j in range(2):
+            for i in range(3):
+                sent(relay.at[j, i], r_send.at[j, i])
             for k in (1, 2, 3):
                 sent(ysend.at[0, 0], y_send.at[j, k])
         sent(column_send, c_send)
@@ -457,6 +503,7 @@
             pltpu.VMEM((NSEL, BS, 2 * S), BF),
             pltpu.VMEM((COLS * 4, 2, BS, BS), BF),
             pltpu.VMEM((COLS * 4, 2, BS, BS), BF),
+            pltpu.VMEM((2, 3, 4, 2, BS, BS), BF),
             pltpu.VMEM((2 * BS, NSEL * BS), BF),
             pltpu.VMEM((2 * S, 8 * BS), BF),
             pltpu.VMEM((BS, 2, S), F32),
@@ -482,6 +529,8 @@
             dma((2, COLS)),
             dma((8,)),
             dma((2, COLS)),
+            dma((2, 3)),
+            dma((2, 3)),
             dma,
             dma,
             dma,

time: 64 us -> 60.7 us (0.948)
  the two profiles are of different devices: /device:TPU:7 before, /device:TPU:1 now
where the time goes in v4:
time: 60.7 us; the launch traced here: 60.6 us
  Pallas kernels  59.3 us (98%)
  between operations  1.29 us (2%)
    pallas_call x1, Pallas kernels, body(): pl.pallas_call(kernel, name='supernode', out_shape=(pltpu.VMEM((BS, 2, S)...  58.4 us

profile of v4, /device:TPU:1, one launch (start us, length us, event | category | flops | bytes accessed | tf_op | source)
XLA Modules:
  0.0 60.6 jit_solution(4118617427425837572)
XLA Ops:
  1.3 58.4 %supernode.1 = (f32[128,2,512]{2,1,0:T(2,128)S(1)}, f32[16,2,512]{2,1,0:T(2,128)S(1)}, f32[16,1,512]{2,1,0:T(1,128)S(1)}, f32[8,128]{1,0:T(8,128)S(1)}) custom-call(bf16[2,1024,512]{2,1,0:T(8,128)(2,1)} %bitcast.11, bf16[64,1024]{1,0:T(8,128)(2,1)} %bitcast.12, f32[16,2,512]{2,1,0:T(2,128)} %bitcast.13, s32[1,16]{1,0:T(1,128)} %ancestors_in.1, ...), custom_call_target="tpu_custom_call" | custom-call | tf_op jit(solution)/shard_map/supernode/pallas_call | solution.py:491
  59.7 0.8 %hand_out.1 = (f32[128,2,512]{2,1,0:T(2,128)}, f32[16,2,512]{2,1,0:T(2,128)}, f32[16,1,512]{2,1,0:T(1,128)}, f32[8,128]{1,0:T(8,128)}) custom-call(f32[128,2,512]{2,1,0:T(2,128)S(1)} %get-tuple-element.12.refs_0_, f32[16,2,512]{2,1,0:T(2,128)S(1)} %get-tuple-element.13.refs_1_, f32[16,1,512]{2,1,0:T(1,128)S(1)} %get-tuple-element.14.refs_2_, ...), custom_call_target="tpu_custom_call" | custom-call | tf_op jit(solution)/shard_map/hand_out/pallas_call | solution.py:566

commit v5 on v4

--- a/solution.py
+++ b/solution.py
@@ -36,6 +36,7 @@
     first_strips,
     second_strips,
     relay,
+    spread,
     abuf,
     left,
     column_send,
@@ -54,6 +55,7 @@
     precv,
     qsend,
     qrecv,
+    beside_sem,
     local_sem,
     l_send,
     l_recv,
@@ -130,29 +132,32 @@
     for copy in small:
         copy.start()
 
-    def piece(rb, z, k):
-        return inverse.at[:, pl.ds((rb * 4 + z) * BS, BS), pl.ds(k * BS, BS)]
+    def piece(rb, z):
+        return inverse.at[:, pl.ds((rb * 4 + z) * BS, BS)]
 
     @pl.when(active)
     def _():
         for j, rb in enumerate(turns):
-            for k in range(4):
-                pltpu.make_async_copy(
-                    piece(rb, depth, k), strips[j].at[col * 4 + k], local_sem.at[6 * j + 1]
-                ).start()
+            pltpu.make_async_copy(
+                piece(rb, depth), strips[j].at[col], local_sem.at[6 * j + 1]
+            ).start()
 
     barrier = pltpu.get_barrier_semaphore()
-    others = [(ds, dz) for ds in (0, 1) for dz in (0, 1, 3, 2) if (ds, dz) != (0, 0)]
-    for ds, dz in others:
-        c = ((side + ds) % 2) * 4 + (depth + dz) % 4
-        pl.semaphore_signal(barrier, inc=1, device_id=(pole, row, c), device_id_type=MESH)
-    for k in (1, 3, 2):
-        pl.semaphore_signal(barrier, inc=1, device_id=(pole, up(k), col), device_id_type=MESH)
-    for k in range(1, POLES):
-        pl.semaphore_signal(
-            barrier, inc=1, device_id=((pole + k) % POLES, row, col), device_id_type=MESH
-        )
-    pl.semaphore_wait(barrier, len(others) + ROWS - 1 + POLES - 1)
+    beside = (((pole + 2) % POLES, row, facing), ((pole + 2) % POLES + 1 - 2 * works, row, facing))
+    neighbours = [
+        (pole, row, facing),
+        (pole, row, at_depth(side, 1)),
+        (pole, row, at_depth(side, 3)),
+        (pole, up(1), col),
+        (pole, up(3), col),
+        (pole + 1 - 2 * works, row, col),
+        *beside,
+    ]
+    for device in neighbours:
+        pl.semaphore_signal(barrier, inc=1, device_id=device, device_id_type=MESH)
+    pl.semaphore_wait(barrier, len(neighbours))
+    for device in beside:
+        pl.semaphore_signal(beside_sem, inc=1, device_id=device, device_id_type=MESH)
     own_factor.wait()
     for copy in small:
         copy.wait()
@@ -164,14 +169,13 @@
         return lbuf.at[r * 4 + c // 2, pl.ds((c % 2) * LROWS + part * HALF, HALF)]
 
     def send_strip(n, j, z):
-        for k in range(4):
-            remote(
-                piece(turns[j], z, k),
-                strips[j].at[col * 4 + k],
-                g_send.at[n],
-                g_recv.at[j, col],
-                (pole, row, works * 4 + z),
-            ).start()
+        remote(
+            piece(turns[j], z),
+            strips[j].at[col],
+            g_send.at[n],
+            g_recv.at[j, col],
+            (pole, row, works * 4 + z),
+        ).start()
 
     @pl.when(jnp.logical_not(active))
     def _():
@@ -181,22 +185,25 @@
         remote(owner.at[side], owner.at[side], o_send, o_recv, (pole, row, facing)).start()
         for j in range(2):
             for i, dz in enumerate((1, 3, 2, 0)):
-                z = (depth + dz) % 4
-                for k in range(4):
-                    remote(
-                        piece(turns[j], z, k),
-                        relay.at[j, i, k] if dz else strips[j].at[col * 4 + k],
-                        g_send.at[4 * j + i],
-                        s_recv.at[j, i] if dz else g_recv.at[j, col],
-                        (pole, row, facing),
-                    ).start()
+                remote(
+                    piece(turns[j], (depth + dz) % 4),
+                    relay.at[j, i] if dz else strips[j].at[col],
+                    g_send.at[4 * j + i],
+                    s_recv.at[j, i] if dz else g_recv.at[j, col],
+                    (pole, row, facing),
+                ).start()
 
     weight_real = table[0, slot[0]]
     weight_imag = table[1, slot[0]]
 
-    def to_position(k):
-        to = (me + k) % GRID
-        return to, (pole, to // COLS, to % COLS)
+    def send_all(src, dst, send, recv):
+        far = [(dr, ds, dz) for dr in range(ROWS) for ds in range(2) for dz in range(4)]
+        far.sort(key=lambda d: -(min(d[0], 4 - d[0]) + d[1] + min(d[2], 4 - d[2])))
+        for dr, ds, dz in far[:-1]:
+            c = at_depth((side + ds) % 2, dz)
+            to = up(dr) * COLS + c
+            remote(src.at[to], dst.at[source], send, recv, (pole, up(dr), c)).start()
+        dst[source] = src[me]
 
     @pl.when(active)
     def _():
@@ -229,10 +236,9 @@
             wait_block(up(1), c)
             send_half(up(1), c, 1, k + 1, (pole, up(3), col))
 
-        def in_plane(c):
-            for dz in (1, 3, 2):
+        def in_plane(c, steps):
+            for dz in steps:
                 send_block(row, c, (pole, row, at_depth(side, dz)))
-            along_rows(c)
 
         def arrived_in_plane(c):
             wait_block(row, c)
@@ -242,7 +248,7 @@
             came(relay.at[j, i], s_recv.at[j, i])
             remote(
                 relay.at[j, i],
-                strips[j].at[pl.ds(facing * 4, 4)],
+                strips[j].at[facing],
                 r_send.at[j, i],
                 g_recv.at[j, facing],
                 (pole, row, at_depth(side, (1, 3, 2)[i])),
@@ -255,28 +261,33 @@
         order = [col, facing]
         for dz in (1, 3, 2):
             order += [at_depth(side, dz), at_depth(1 - side, dz)]
-        in_plane(col)
+        in_plane(col, (1, 3))
+        along_rows(col)
         send_own(0, 0)
         send_own(0, 1)
+        arrived_in_plane(order[2])
+        in_plane(col, (2,))
         wait_block(row, facing)
-        in_plane(facing)
-        arrived_in_plane(order[2])
+        in_plane(facing, (1, 3, 2))
+        along_rows(facing)
+        send_own(0, 2)
         arrived_in_plane(order[4])
         forward(0, 0)
         forward(0, 1)
-        send_own(0, 2)
+        send_own(1, 0)
+        send_own(1, 1)
         for k in (3, 5, 6, 7):
             arrived_in_plane(order[k])
         forward(0, 2)
-        send_own(1, 0)
-        send_own(1, 1)
-        for k in (0, 1, 2, 4):
+        send_own(1, 2)
+        for k in (0, 1, 2):
             pass_on(order[k])
         forward(1, 0)
-        send_own(1, 2)
-        for k in (3, 5, 6, 7):
+        for k in (4, 3):
             pass_on(order[k])
         forward(1, 1)
+        for k in (5, 6, 7):
+            pass_on(order[k])
 
         came(owner.at[0], o_recv)
         lane = lax.broadcasted_iota(jnp.int32, (64, 512), 1)
@@ -289,8 +300,8 @@
             target = jnp.where(across == down, owner[s].astype(F32), 0.0)
             target = jnp.sum(target, axis=1, keepdims=True).astype(jnp.int32)
             target = ((target & 31) * 32 + (target >> 5) * 8).astype(F32)
-            spread = jnp.where(named == owner_index, target, 0.0)
-            key = jnp.sum(spread, axis=0, keepdims=True) + (lane[:1] & 7).astype(F32)
+            placed = jnp.where(named == owner_index, target, 0.0)
+            key = jnp.sum(placed, axis=0, keepdims=True) + (lane[:1] & 7).astype(F32)
             pick[:, s * 512 : (s + 1) * 512] = jnp.where(position == key, 1.0, 0.0).astype(BF)
 
         forward(1, 2)
@@ -310,19 +321,19 @@
         shares = [None, None]
         columns = []
         for j, rb in enumerate(turns):
-            for s in (0, 1):
-                for dz in (1, 3, 2, 0):
-                    c = at_depth(s, dz)
-
-                    @pl.when(c != col)
-                    def _():
-                        came(strips[j].at[pl.ds(0, 4)], g_recv.at[j, c])
-
-            own = strips[j].at[pl.ds(col * 4, 4)]
-            pltpu.make_async_copy(own, own, local_sem.at[6 * j + 1]).wait()
+            for ds, dz in ((0, 0), (0, 1), (0, 3), (0, 2), (1, 1), (1, 3), (1, 0), (1, 2)):
+                c = at_depth((side + ds) % 2, dz)
+                if (ds, dz) == (0, 0):
+                    own = strips[j].at[c]
+                    pltpu.make_async_copy(own, own, local_sem.at[6 * j + 1]).wait()
+                else:
+                    came(strips[j].at[0], g_recv.at[j, c])
+                for part in range(2):
+                    for k in range(4):
+                        spread[c * 4 + k, part] = strips[j][c, part, :, k * BS : (k + 1) * BS]
             for i in range(NSEL):
                 for part in range(2):
-                    abuf[part * BS : (part + 1) * BS, i * BS : (i + 1) * BS] = strips[j][
+                    abuf[part * BS : (part + 1) * BS, i * BS : (i + 1) * BS] = spread[
                         ancestors[0, i], part
                     ]
             acc = jnp.dot(
@@ -374,13 +385,7 @@
         tiles = tiles[:, :BS] + tiles[:, BS:]
         tsend[...] = tiles.astype(BF).reshape(GRID, 32, BS)
 
-        def send_tiles(k, carry):
-            to, device = to_position(k)
-            remote(tsend.at[to], trecv.at[source], t_send, t_recv, device).start()
-            return carry
-
-        lax.fori_loop(1, GRID, send_tiles, 0)
-        trecv[source] = tsend[me]
+        send_all(tsend, trecv, t_send, t_recv)
 
         for k in (1, 3, 2):
             for rb in range(2):
@@ -396,13 +401,7 @@
             .reshape(GRID, S // GRID, 2 * BS)
         )
 
-        def send_diag(k, carry):
-            to, device = to_position(k)
-            remote(dsend.at[to], drecv.at[source], d_send, d_recv, device).start()
-            return carry
-
-        lax.fori_loop(1, GRID, send_diag, 0)
-        drecv[source] = dsend[me]
+        send_all(dsend, drecv, d_send, d_recv)
 
     def arrivals(ref, recv):
         @pl.when(active)
@@ -416,6 +415,7 @@
     arrivals(trecv, t_recv)
     total = jnp.sum(trecv[...].astype(F32), axis=0)
     psend[...] = total.reshape(POLES, 8, BS)
+    pl.semaphore_wait(beside_sem, len(beside))
     for k in range(1, POLES):
         p = (pole + k) % POLES
         remote(psend.at[p], precv.at[pole], p_send.at[k], p_recv.at[pole], (p, row, col)).start()
@@ -446,7 +446,7 @@
         sent(lbuf.at[0, pl.ds(0, LROWS)], l_send.at[0])
         sent(owner.at[0], o_send)
         for n in range(8):
-            sent(first_strips.at[pl.ds(0, 4)], g_send.at[n])
+            sent(first_strips.at[0], g_send.at[n])
         came(column_out, c_recv)
 
     @pl.when(active)
@@ -456,7 +456,7 @@
         for n in range(16):
             sent(lbuf.at[0, pl.ds(0, HALF)], h_send.at[n])
         for n in range(6):
-            sent(first_strips.at[pl.ds(0, 4)], g_send.at[n])
+            sent(first_strips.at[0], g_send.at[n])
         for j in range(2):
             for i in range(3):
                 sent(relay.at[j, i], r_send.at[j, i])
@@ -501,9 +501,10 @@
         out_specs=(vmem,) * 4,
         scratch_shapes=[
             pltpu.VMEM((NSEL, BS, 2 * S), BF),
+            pltpu.VMEM((COLS, 2, BS, S), BF),
+            pltpu.VMEM((COLS, 2, BS, S), BF),
+            pltpu.VMEM((2, 3, 2, BS, S), BF),
             pltpu.VMEM((COLS * 4, 2, BS, BS), BF),
-            pltpu.VMEM((COLS * 4, 2, BS, BS), BF),
-            pltpu.VMEM((2, 3, 4, 2, BS, BS), BF),
             pltpu.VMEM((2 * BS, NSEL * BS), BF),
             pltpu.VMEM((2 * S, 8 * BS), BF),
             pltpu.VMEM((BS, 2, S), F32),
@@ -522,6 +523,7 @@
             pltpu.VMEM((POLES, 8, BS), F32),
             pltpu.VMEM((S // GRID, S), F32),
             pltpu.VMEM((POLES, S // GRID, S), F32),
+            pltpu.SemaphoreType.REGULAR,
             dma((8,)),
             dma((22,)),
             dma((GRID,)),

time: 60.7 us -> 59.2 us (0.975)
  Pallas kernels: 59.3 us -> 57.8 us
    pallas_call x1, Pallas kernels: 58.4 us -> 56.9 us  [body(): pl.pallas_call(kernel, name='supernode', out_shape=(pltpu.VMEM((BS, 2, S)...]
where the time goes in v5:
time: 59.2 us; the launch traced here: 59 us
  Pallas kernels  57.8 us (98%)
  between operations  1.29 us (2%)
    pallas_call x1, Pallas kernels, body(): pl.pallas_call(kernel, name='supernode', out_shape=(pltpu.VMEM((BS, 2, S)...  56.9 us

profile of v5, /device:TPU:1, one launch (start us, length us, event | category | flops | bytes accessed | tf_op | source)
XLA Modules:
  0.0 59.0 jit_solution(15285487468697145759)
XLA Ops:
  1.3 56.9 %supernode.1 = (f32[128,2,512]{2,1,0:T(2,128)S(1)}, f32[16,2,512]{2,1,0:T(2,128)S(1)}, f32[16,1,512]{2,1,0:T(1,128)S(1)}, f32[8,128]{1,0:T(8,128)S(1)}) custom-call(bf16[2,1024,512]{2,1,0:T(8,128)(2,1)} %bitcast.11, bf16[64,1024]{1,0:T(8,128)(2,1)} %bitcast.12, f32[16,2,512]{2,1,0:T(2,128)} %bitcast.13, s32[1,16]{1,0:T(1,128)} %ancestors_in.1, ...), custom_call_target="tpu_custom_call" | custom-call | tf_op jit(solution)/shard_map/supernode/pallas_call | solution.py:491
  58.2 0.8 %hand_out.1 = (f32[128,2,512]{2,1,0:T(2,128)}, f32[16,2,512]{2,1,0:T(2,128)}, f32[16,1,512]{2,1,0:T(1,128)}, f32[8,128]{1,0:T(8,128)}) custom-call(f32[128,2,512]{2,1,0:T(2,128)S(1)} %get-tuple-element.12.refs_0_, f32[16,2,512]{2,1,0:T(2,128)S(1)} %get-tuple-element.13.refs_1_, f32[16,1,512]{2,1,0:T(1,128)S(1)} %get-tuple-element.14.refs_2_, ...), custom_call_target="tpu_custom_call" | custom-call | tf_op jit(solution)/shard_map/hand_out/pallas_call | solution.py:568

commit v6 on v5

--- a/solution.py
+++ b/solution.py
@@ -83,7 +83,8 @@
     pole, row, col = lax.axis_index("pole"), lax.axis_index("row"), lax.axis_index("col")
     side, depth = col // 4, col % 4
     me = row * COLS + col
-    works = pole % 2
+    core = pole % 2
+    works = 1 - core
     active = side == works
     facing = (1 - side) * 4 + depth
     source = row * 4 + depth
@@ -143,14 +144,14 @@
             ).start()
 
     barrier = pltpu.get_barrier_semaphore()
-    beside = (((pole + 2) % POLES, row, facing), ((pole + 2) % POLES + 1 - 2 * works, row, facing))
+    beside = (((pole + 2) % POLES, row, facing), ((pole + 2) % POLES + 1 - 2 * core, row, facing))
     neighbours = [
         (pole, row, facing),
         (pole, row, at_depth(side, 1)),
         (pole, row, at_depth(side, 3)),
         (pole, up(1), col),
         (pole, up(3), col),
-        (pole + 1 - 2 * works, row, col),
+        (pole + 1 - 2 * core, row, col),
         *beside,
     ]
     for device in neighbours:
@@ -430,7 +431,7 @@
     dreal = jnp.concatenate(dreal, axis=1) + dinv[:, 0, :]
     dimag = jnp.concatenate(dimag, axis=1) + dinv[:, 1, :]
     qsend[...] = weight_real * dimag + weight_imag * dreal
-    for k in range(1, POLES):
+    for k in (2, 3, 1):
         p = (pole + k) % POLES
         remote(qsend, qrecv.at[pole], q_send.at[k], q_recv.at[pole], (p, row, col)).start()
     qrecv[pole] = qsend[...]

time: 59.2 us -> 60 us (1.014)
  Pallas kernels: 57.8 us -> 58.6 us
    pallas_call x1, Pallas kernels: 56.9 us -> 57.8 us  [body(): pl.pallas_call(kernel, name='supernode', out_shape=(pltpu.VMEM((BS, 2, S)...]
where the time goes in v6:
time: 60 us; the launch traced here: 59.9 us
  Pallas kernels  58.6 us (98%)
  between operations  1.29 us (2%)
    pallas_call x1, Pallas kernels, body(): pl.pallas_call(kernel, name='supernode', out_shape=(pltpu.VMEM((BS, 2, S)...  57.8 us

profile of v6, /device:TPU:1, one launch (start us, length us, event | category | flops | bytes accessed | tf_op | source)
XLA Modules:
  0.0 59.9 jit_solution(12125429276808968496)
XLA Ops:
  1.3 57.8 %supernode.1 = (f32[128,2,512]{2,1,0:T(2,128)S(1)}, f32[16,2,512]{2,1,0:T(2,128)S(1)}, f32[16,1,512]{2,1,0:T(1,128)S(1)}, f32[8,128]{1,0:T(8,128)S(1)}) custom-call(bf16[2,1024,512]{2,1,0:T(8,128)(2,1)} %bitcast.11, bf16[64,1024]{1,0:T(8,128)(2,1)} %bitcast.12, f32[16,2,512]{2,1,0:T(2,128)} %bitcast.13, s32[1,16]{1,0:T(1,128)} %ancestors_in.1, ...), custom_call_target="tpu_custom_call" | custom-call | tf_op jit(solution)/shard_map/supernode/pallas_call | solution.py:492
  59.1 0.8 %hand_out.1 = (f32[128,2,512]{2,1,0:T(2,128)}, f32[16,2,512]{2,1,0:T(2,128)}, f32[16,1,512]{2,1,0:T(1,128)}, f32[8,128]{1,0:T(8,128)}) custom-call(f32[128,2,512]{2,1,0:T(2,128)S(1)} %get-tuple-element.12.refs_0_, f32[16,2,512]{2,1,0:T(2,128)S(1)} %get-tuple-element.13.refs_1_, f32[16,1,512]{2,1,0:T(1,128)S(1)} %get-tuple-element.14.refs_2_, ...), custom_call_target="tpu_custom_call" | custom-call | tf_op jit(solution)/shard_map/hand_out/pallas_call | solution.py:569

commit v7 on v5

--- a/solution.py
+++ b/solution.py
@@ -198,7 +198,7 @@
 
     def send_all(src, dst, send, recv):
         far = [(dr, ds, dz) for dr in range(ROWS) for ds in range(2) for dz in range(4)]
-        far.sort(key=lambda d: -(min(d[0], 4 - d[0]) + d[1] + min(d[2], 4 - d[2])))
+        far.sort(key=lambda d: (-min(d[2], 4 - d[2]), -d[1], -min(d[0], 4 - d[0])))
         for dr, ds, dz in far[:-1]:
             c = at_depth((side + ds) % 2, dz)
             to = up(dr) * COLS + c

time: 59.2 us -> 59.2 us (level)
  no operation moved by 1% of the time
where the time goes in v7:
time: 59.2 us; the launch traced here: 59.1 us
  Pallas kernels  57.8 us (98%)
  between operations  1.29 us (2%)
    pallas_call x1, Pallas kernels, body(): pl.pallas_call(kernel, name='supernode', out_shape=(pltpu.VMEM((BS, 2, S)...  56.9 us

profile of v7, /device:TPU:1, one launch (start us, length us, event | category | flops | bytes accessed | tf_op | source)
XLA Modules:
  0.0 59.1 jit_solution(6510371751390656815)
XLA Ops:
  1.3 56.9 %supernode.1 = (f32[128,2,512]{2,1,0:T(2,128)S(1)}, f32[16,2,512]{2,1,0:T(2,128)S(1)}, f32[16,1,512]{2,1,0:T(1,128)S(1)}, f32[8,128]{1,0:T(8,128)S(1)}) custom-call(bf16[2,1024,512]{2,1,0:T(8,128)(2,1)} %bitcast.11, bf16[64,1024]{1,0:T(8,128)(2,1)} %bitcast.12, f32[16,2,512]{2,1,0:T(2,128)} %bitcast.13, s32[1,16]{1,0:T(1,128)} %ancestors_in.1, ...), custom_call_target="tpu_custom_call" | custom-call | tf_op jit(solution)/shard_map/supernode/pallas_call | solution.py:491
  58.2 0.8 %hand_out.1 = (f32[128,2,512]{2,1,0:T(2,128)}, f32[16,2,512]{2,1,0:T(2,128)}, f32[16,1,512]{2,1,0:T(1,128)}, f32[8,128]{1,0:T(8,128)}) custom-call(f32[128,2,512]{2,1,0:T(2,128)S(1)} %get-tuple-element.12.refs_0_, f32[16,2,512]{2,1,0:T(2,128)S(1)} %get-tuple-element.13.refs_1_, f32[16,1,512]{2,1,0:T(1,128)S(1)} %get-tuple-element.14.refs_2_, ...), custom_call_target="tpu_custom_call" | custom-call | tf_op jit(solution)/shard_map/hand_out/pallas_call | solution.py:568
